TPU v7x, 256 devices: a whole 4x4x8 slice. The times are simulated.
256 devices in a mesh: grp: 16 (over x, y_hi, core), mem: 16 (over z, y_lo).
Axes of the slice: x: 4, y: 4 (y_hi: 2, y_lo: 2; y = y_hi * 2 + y_lo), z: 8, core: 2. Of those that a mesh axis runs over, the one named last changes fastest.
Arguments:
- residual: float32 [2048, 64, 256], P(('grp', 'mem')), may hold values from -6 to 6
- direction: float32 [2048, 64, 256], P(('grp', 'mem')), may hold values from -6 to 6
- local_inverse: bfloat16 [2048, 256, 256], P(('grp', 'mem')), may hold values from -1 to 16, as said below
- dirichlet: bfloat16 [2048, 256, 256], P(('grp', 'mem')), may hold values from -1 to 16, as said below
- coupling: bfloat16 [2048, 24, 256], P(('grp', 'mem')), may hold values from -0.375 to 0.375
- corner_map: int32 [2048, 24], P(('grp', 'mem')), may hold values from 0 to 6143
- coarse_factor: bfloat16 [16, 2048, 2048], P('grp'), may hold values from -1 to 3, as said below
Outputs:
- new_residual: float32 [2048, 64, 256], P(('grp', 'mem'))
- new_direction: float32 [2048, 64, 256], P(('grp', 'mem'))
- step_sizes: float32 [3, 64], replicated
Inputs may be any that keep to these rules, and one draw needn't show every extreme that they name: `local_inverse`: each subdomain's matrix is symmetric positive definite. `dirichlet`: each subdomain's matrix is symmetric positive definite. `coarse_factor`: each group's factor is lower triangular with a positive diagonal.
All inputs are finite; a program needn't handle non-finite values.
Results may differ from a plain program's by a relative error of at most 0.0083.
Values sent between devices are 32-bit elements; how exact they have to be, the bound alone decides.
A program may use at most 128 MiB of HBM per device.

v0:
```python
import functools

import jax
import jax.numpy as jnp
from jax import lax
from jax.sharding import Mesh
from jax.sharding import PartitionSpec as P

ITERS = 3
GRP = ("grp_0", "grp_1", "grp_2")
GRP_MEM = ("grp_0", "grp_1", "grp_2", "mem_0", "mem_1")
MEM = ("mem_0", "mem_1")


highest = lax.Precision.HIGHEST


def from_behind(block, axis, distance):
    devices = range(lax.axis_size(axis))
    route = [((i - distance) % len(devices), i) for i in devices]
    return lax.ppermute(block, axis, route)


def by_axis(x, axes):
    return functools.reduce(lax.psum, axes, x)


def cut_along(x, dim, count):
    lengths = x.shape
    tiles = x.reshape(*lengths[:dim], count, lengths[dim] // count, *lengths[dim + 1 :])
    return jnp.moveaxis(tiles, dim, 0)


def summed_on_arrival(x, axis, dim):
    count = lax.axis_size(axis)
    tiles = lax.all_to_all(cut_along(x, dim, count), axis, 0, 0, tiled=True)
    return jnp.sum(tiles, axis=0)


def joined_along(tiles, dim):
    lengths = list(tiles.shape[1:])
    lengths[dim] *= tiles.shape[0]
    return jnp.moveaxis(tiles, 0, dim).reshape(lengths)


def sent_to_all(x, axis):
    count = lax.axis_size(axis)
    return lax.all_to_all(jnp.broadcast_to(x[None], (count, *x.shape)), axis, 0, 0, tiled=True)


def collect(x, axis, dim):
    return joined_along(sent_to_all(x, axis), dim)


def extended(cells, sides, width):
    for axis, dim in sides:
        count = lax.axis_size(axis)
        head = lax.slice_in_dim(cells, 0, width, axis=dim)
        tail = lax.slice_in_dim(cells, cells.shape[dim] - width, cells.shape[dim], axis=dim)
        cells = jnp.concatenate(
            [
                lax.ppermute(tail, axis, [(i, (i + 1) % count) for i in range(count)]),
                cells,
                lax.ppermute(head, axis, [((i + 1) % count, i) for i in range(count)]),
            ],
            axis=dim,
        )
    return cells


def solve_local(matrices, vectors):
    return jnp.einsum(
        "sij,skj->ski", matrices, vectors.astype(jnp.bfloat16), preferred_element_type=jnp.float32
    )


def column_sums(left_side, right_side):
    return jnp.sum(left_side * right_side, axis=(0, 2))


def coarse_solve(factor, coarse_load):
    forward = jax.scipy.linalg.solve_triangular(factor, coarse_load.T, lower=True)
    return jax.scipy.linalg.solve_triangular(factor, forward, lower=True, trans=1).T


def fold_neighbours(partial_value, block_size):
    from_upper = from_behind(partial_value[:, :block_size], GRP, -1)
    from_lower = from_behind(partial_value[:, 2 * block_size :], GRP, 1)
    return partial_value[:, block_size : 2 * block_size] + from_upper + from_lower


def local(residual, direction, local_inverse, dirichlet, coupling, corner_map, coarse_factor):
    sub_count, rhs_count, dofs_count = residual.shape
    corner_count = coupling.shape[1]
    block_size = coarse_factor.shape[1]
    factor = coarse_factor[0].astype(jnp.float32)
    flat_map = corner_map.reshape(-1)
    coupling_wide = coupling.astype(jnp.float32)
    precond = solve_local(dirichlet, residual)
    norm_now = by_axis(column_sums(residual, precond), GRP_MEM)
    step_list = []
    for iteration in range(ITERS):
        solved = solve_local(local_inverse, direction)
        partial_corner = jnp.einsum("ski,sci->skc", solved, coupling_wide, precision=highest)
        flat_corner = partial_corner.transpose(1, 0, 2).reshape(rhs_count, sub_count * corner_count)
        partial_value = (
            jnp.zeros((rhs_count, 3 * block_size), jnp.float32).at[:, flat_map].add(flat_corner)
        )
        folded = fold_neighbours(partial_value, block_size)
        column_load = summed_on_arrival(folded, MEM, 0)
        solution = collect(coarse_solve(factor, column_load), MEM, 0)
        widened = extended(solution, ((GRP, 1),), block_size)
        picked = widened[:, flat_map].reshape(rhs_count, sub_count, corner_count).transpose(1, 0, 2)
        lifted = jnp.einsum("skc,sci->ski", picked, coupling_wide, precision=highest)
        image = solve_local(local_inverse, direction + lifted)
        curvature = by_axis(column_sums(direction, image), GRP_MEM)
        alpha = norm_now / curvature
        step_list.append(alpha)
        residual = residual - alpha[None, :, None] * image
        precond = solve_local(dirichlet, residual)
        norm_next = by_axis(column_sums(residual, precond), GRP_MEM)
        direction = precond + (norm_next / norm_now)[None, :, None] * direction
        norm_now = norm_next
    return (residual, direction, jnp.stack(step_list))


def solution(mesh):
    finer = Mesh(mesh.devices.reshape(4, 2, 2, 8, 2), ("grp_0", "grp_1", "grp_2", "mem_0", "mem_1"))
    return jax.shard_map(
        local,
        mesh=finer,
        in_specs=(
            P(GRP_MEM, None, None),
            P(GRP_MEM, None, None),
            P(GRP_MEM, None, None),
            P(GRP_MEM, None, None),
            P(GRP_MEM, None, None),
            P(GRP_MEM, None),
            P(GRP, None, None),
        ),
        out_specs=(P(GRP_MEM, None, None), P(GRP_MEM, None, None), P()),
        check_vma=False,
    )
```

profile of v0, /device:TPU:1, one launch (start us, length us, event | category | flops | bytes accessed | tf_op | source)
XLA Modules:
  0.0 912.0 jit_solution(1506131766933078527)
XLA Ops:
  4.6 3.0 scatter_custom_fusion
  7.7 3.0 fusion.320
  13.0 4.3 collective-permute-start.1
  18.4 11.2 %convert_select_fusion = f32[2048,2048]{1,0:T(8,128)} fusion(bf16[1,2048,2048]{2,1,0:T(8,128)(2,1)} %param.17), kind=kLoop, calls=%fused_computation.8 | loop fusion | flops 12582912 | bytes 25165824 | tf_op jit(solution)/shard_map/jit(_solve_triangular)/triangular_solve | solution.py:83
  30.7 2.9 collective-permute-done
  36.1 7.6 all-to-all-start
  43.7 56.9 %while.12 = (s32[]{:T(128)}, f32[2048,2048]{1,0:T(8,128)}, s32[16,2]{0,1:T(2,128)S(1)}, f32[16,128,128]{2,1,0:T(8,128)}, s32[]{:T(128)}) while((s32[]{:T(128)}, f32[2048,2048]{1,0:T(8,128)}, s32[16,2]{0,1:T(2,128)S(1)}, f32[16,128,128]{2,1,0:T(8,128)}, s32[]{:T(128)}) %tuple.417), condition=%wide.while_cond.1, body=%wide.while_body.1.sunk | while | flops 2 | bytes 132205 | solution.py:83
  51.5 2.9 bitcast_dynamic-update-slice_fusion.2
  62.2 2.9 bitcast_dynamic-update-slice_fusion.2
  72.9 2.9 bitcast_dynamic-update-slice_fusion.2
  80.0 2.9 bitcast_dynamic-update-slice_fusion.2
  90.7 2.9 bitcast_dynamic-update-slice_fusion.2
  100.6 158.1 %custom-call.11 = f32[16,128,128]{1,2,0:T(8,128)S(1)} custom-call(f32[16,128,128]{2,1,0:T(8,128)} %get-tuple-element.46), custom_call_target="InvertDiagBlocksLowerTriangular" | custom-call | tf_op jit(solution)/shard_map/jit(_solve_triangular)/triangular_solve | solution.py:83
  313.4 21.9 %all_to_all.30 = f32[16,4,2048]{2,1,0:T(4,128)} all-to-all(f32[16,4,2048]{2,1,0:T(4,128)S(1)} %broadcast_in_dim.6), channel_id=1, replica_groups=mesh['grp_0'=4,'grp_1'=2,'grp_2'=2,'mem_0'=8,'mem_1'=2] {'mem_0','mem_1'}, dimensions={0} | all-to-all | bytes 1048576 | tf_op jit(solution)/shard_map/all_to_all | solution.py:48
  337.3 3.8 collective-permute-start.3
  345.8 8.6 collective-permute-done.3
  359.2 3.7 pad_maximum_fusion
  369.4 7.5 all-reduce.1
  376.8 5.3 all-reduce.4
  382.1 3.0 all-reduce.3
  385.1 10.9 %all-reduce = (f32[64]{0:T(128)S(1)}, f32[64]{0:T(128)S(1)}) all-reduce(f32[64]{0:T(128)S(1)} %get-tuple-element.65, f32[64]{0:T(128)S(1)} %get-tuple-element.66), channel_id=1, replica_groups=mesh['grp_0'=4,'grp_1'=2,'grp_2'=2,'mem_0'=8,'mem_1'=2] {'mem_0'}, use_global_device_ids=true, to_apply=%region_4.0 | all-reduce | flops 128 | bytes 1024 | tf_op jit(solution)/shard_map/psum | solution.py:25
  396.0 3.8 all-reduce.2
  403.3 6.0 psum.255
  409.3 5.6 psum.256
  414.8 10.0 %psum.257 = f32[64]{0:T(128)S(1)} all-reduce(f32[64]{0:T(128)S(1)} %psum.256), channel_id=1, replica_groups=mesh['grp_0'=4,'grp_1'=2,'grp_2'=2,'mem_0'=8,'mem_1'=2] {'grp_2'}, use_global_device_ids=true, to_apply=%region_17.0 | all-reduce | flops 64 | bytes 512 | tf_op jit(solution)/shard_map/psum | solution.py:25
  424.8 11.8 %psum.258 = f32[64]{0:T(128)S(1)} all-reduce(f32[64]{0:T(128)S(1)} %psum.257), channel_id=1, replica_groups=mesh['grp_0'=4,'grp_1'=2,'grp_2'=2,'mem_0'=8,'mem_1'=2] {'mem_0'}, use_global_device_ids=true, to_apply=%region_18.0 | all-reduce | flops 64 | bytes 512 | tf_op jit(solution)/shard_map/psum | solution.py:25
  436.6 3.8 psum.259
  443.3 3.0 scatter_custom_fusion.1
  446.4 3.6 fusion.319
  454.7 8.4 collective-permute-start.5
  465.5 9.7 %collective-permute-done.5 = f32[64,2048]{1,0:T(8,128)} collective-permute-done((f32[64,2048]{1,0:T(8,128)}, f32[64,2048]{1,0:T(8,128)}, u32[]{:S(2)}, u32[]{:S(2)}) %collective-permute-start.5) | collective-permute-done | bytes 524320 | tf_op jit(solution)/shard_map/ppermute | solution.py:21
  481.6 18.0 %all_to_all.31 = f32[16,4,2048]{2,1,0:T(4,128)} all-to-all(f32[16,4,2048]{2,1,0:T(4,128)} %reshape.154), channel_id=1, replica_groups=mesh['grp_0'=4,'grp_1'=2,'grp_2'=2,'mem_0'=8,'mem_1'=2] {'mem_0','mem_1'}, dimensions={0} | all-to-all | bytes 1048576 | tf_op jit(solution)/shard_map/all_to_all | solution.py:36
  554.2 18.7 %all_to_all.32 = f32[16,4,2048]{2,1,0:T(4,128)} all-to-all(f32[16,4,2048]{2,1,0:T(4,128)S(1)} %broadcast_in_dim.7), channel_id=1, replica_groups=mesh['grp_0'=4,'grp_1'=2,'grp_2'=2,'mem_0'=8,'mem_1'=2] {'mem_0','mem_1'}, dimensions={0} | all-to-all | bytes 1048576 | tf_op jit(solution)/shard_map/all_to_all | solution.py:48
  574.9 3.2 collective-permute-start.6
  580.5 10.4 %collective-permute-done.7 = f32[64,2048]{1,0:T(8,128)} collective-permute-done((f32[64,2048]{1,0:T(8,128)}, f32[64,2048]{1,0:T(8,128)}, u32[]{:S(2)}, u32[]{:S(2)}) %collective-permute-start.7) | collective-permute-done | bytes 524320 | tf_op jit(solution)/shard_map/ppermute | solution.py:64
  595.7 3.7 pad_maximum_fusion.1
  605.8 6.0 psum.260
  611.8 5.3 psum.261
  619.6 10.9 %psum.263 = f32[64]{0:T(128)S(1)} all-reduce(f32[64]{0:T(128)S(1)} %psum.262), channel_id=1, replica_groups=mesh['grp_0'=4,'grp_1'=2,'grp_2'=2,'mem_0'=8,'mem_1'=2] {'mem_0'}, use_global_device_ids=true, to_apply=%region_26.0 | all-reduce | flops 64 | bytes 512 | tf_op jit(solution)/shard_map/psum | solution.py:25
  630.5 3.8 psum.264
  637.7 7.4 psum.265
  645.1 5.3 psum.266
  650.4 10.4 %psum.267 = f32[64]{0:T(128)S(1)} all-reduce(f32[64]{0:T(128)S(1)} %psum.266), channel_id=1, replica_groups=mesh['grp_0'=4,'grp_1'=2,'grp_2'=2,'mem_0'=8,'mem_1'=2] {'grp_2'}, use_global_device_ids=true, to_apply=%region_31.0 | all-reduce | flops 64 | bytes 512 | tf_op jit(solution)/shard_map/psum | solution.py:25
  660.8 11.9 %psum.268 = f32[64]{0:T(128)S(1)} all-reduce(f32[64]{0:T(128)S(1)} %psum.267), channel_id=1, replica_groups=mesh['grp_0'=4,'grp_1'=2,'grp_2'=2,'mem_0'=8,'mem_1'=2] {'mem_0'}, use_global_device_ids=true, to_apply=%region_32.0 | all-reduce | flops 64 | bytes 512 | tf_op jit(solution)/shard_map/psum | solution.py:25
  672.6 3.8 psum.269
  679.3 3.0 scatter_custom_fusion.2
  682.4 3.7 fusion.318
  690.7 8.1 collective-permute-start.9
  701.2 9.7 %collective-permute-done.9 = f32[64,2048]{1,0:T(8,128)} collective-permute-done((f32[64,2048]{1,0:T(8,128)}, f32[64,2048]{1,0:T(8,128)}, u32[]{:S(2)}, u32[]{:S(2)}) %collective-permute-start.9) | collective-permute-done | bytes 524320 | tf_op jit(solution)/shard_map/ppermute | solution.py:21
  717.7 17.5 %all_to_all.33 = f32[16,4,2048]{2,1,0:T(4,128)} all-to-all(f32[16,4,2048]{2,1,0:T(4,128)} %reshape.158), channel_id=1, replica_groups=mesh['grp_0'=4,'grp_1'=2,'grp_2'=2,'mem_0'=8,'mem_1'=2] {'mem_0','mem_1'}, dimensions={0} | all-to-all | bytes 1048576 | tf_op jit(solution)/shard_map/all_to_all | solution.py:36
  789.8 18.3 %all_to_all.34 = f32[16,4,2048]{2,1,0:T(4,128)S(1)} all-to-all(f32[16,4,2048]{2,1,0:T(4,128)S(1)} %broadcast_in_dim.8), channel_id=1, replica_groups=mesh['grp_0'=4,'grp_1'=2,'grp_2'=2,'mem_0'=8,'mem_1'=2] {'mem_0','mem_1'}, dimensions={0} | all-to-all | bytes 1048576 | tf_op jit(solution)/shard_map/all_to_all | solution.py:48
  809.0 3.2 collective-permute-start.10
  813.7 11.4 %collective-permute-done.11 = f32[64,2048]{1,0:T(8,128)} collective-permute-done((f32[64,2048]{1,0:T(8,128)}, f32[64,2048]{1,0:T(8,128)}, u32[]{:S(2)}, u32[]{:S(2)}) %collective-permute-start.11) | collective-permute-done | bytes 524320 | tf_op jit(solution)/shard_map/ppermute | solution.py:64
  829.8 3.4 pad_maximum_fusion.2
  838.9 6.0 psum.270
  844.9 5.3 psum.271
  850.1 5.3 psum.272
  855.4 11.0 %psum.273 = f32[64]{0:T(128)S(1)} all-reduce(f32[64]{0:T(128)S(1)} %psum.272), channel_id=1, replica_groups=mesh['grp_0'=4,'grp_1'=2,'grp_2'=2,'mem_0'=8,'mem_1'=2] {'mem_0'}, use_global_device_ids=true, to_apply=%region_40.0 | all-reduce | flops 64 | bytes 512 | tf_op jit(solution)/shard_map/psum | solution.py:25
  866.5 3.8 psum.274
  872.0 6.0 psum.275
  878.0 5.6 psum.276
  883.5 9.7 %psum.277 = f32[64]{0:T(128)S(1)} all-reduce(f32[64]{0:T(128)S(1)} %psum.276), channel_id=1, replica_groups=mesh['grp_0'=4,'grp_1'=2,'grp_2'=2,'mem_0'=8,'mem_1'=2] {'grp_2'}, use_global_device_ids=true, to_apply=%region_45.0 | all-reduce | flops 64 | bytes 512 | tf_op jit(solution)/shard_map/psum | solution.py:25
  893.2 12.0 %psum.278 = f32[64]{0:T(128)S(1)} all-reduce(f32[64]{0:T(128)S(1)} %psum.277), channel_id=1, replica_groups=mesh['grp_0'=4,'grp_1'=2,'grp_2'=2,'mem_0'=8,'mem_1'=2] {'mem_0'}, use_global_device_ids=true, to_apply=%region_46.0 | all-reduce | flops 64 | bytes 512 | tf_op jit(solution)/shard_map/psum | solution.py:25
  905.2 3.8 psum.279
  (672 shorter events, 308.6 us)
Async XLA Ops:
  0.6 1.2 copy-start
  13.0 17.7 %collective-permute-start.1 = (f32[64,2048]{1,0:T(8,128)}, f32[64,2048]{1,0:T(8,128)}, u32[]{:S(2)}, u32[]{:S(2)}) collective-permute-start(f32[64,2048]{1,0:T(8,128)} %copy.51), channel_id=1, source_target_pairs={{240,0},{0,16},{16,32},{32,48},{48,64},{64,80},{80,96},{96,112},{1... | collective-permute-start | bytes 1572872 | tf_op jit(solution)/shard_map/ppermute | solution.py:21
  18.4 15.3 %collective-permute-start = (f32[64,2048]{1,0:T(8,128)}, f32[64,2048]{1,0:T(8,128)}, u32[]{:S(2)}, u32[]{:S(2)}) collective-permute-start(f32[64,2048]{1,0:T(8,128)} %copy.50), channel_id=1, source_target_pairs={{16,0},{32,16},{48,32},{64,48},{80,64},{96,80},{112,96},{128,112},... | collective-permute-start | bytes 1572872 | tf_op jit(solution)/shard_map/ppermute | solution.py:21
  29.6 312.0 %copy-start.1 = (bf16[8,256,256]{2,1,0:T(8,128)(2,1)S(1)}, bf16[8,256,256]{2,1,0:T(8,128)(2,1)}, u32[]{:S(2)}) copy-start(bf16[8,256,256]{2,1,0:T(8,128)(2,1)} %param.14) | copy-start | bytes 3145732
  36.1 222.7 %all-to-all-start = ((f32[16,4,2048]{2,1,0:T(4,128)}), f32[16,4,2048]{2,1,0:T(4,128)}, u32[]{:S(2)}, u32[]{:S(2)}) async-start(f32[16,4,2048]{2,1,0:T(4,128)} %reshape.150), calls=%async_computation | async-start | bytes 1048576 | tf_op jit(solution)/shard_map/all_to_all | solution.py:36
  267.1 98.4 %copy-start.6 = (bf16[8,24,256]{2,1,0:T(8,128)(2,1)S(1)}, bf16[8,24,256]{2,1,0:T(8,128)(2,1)}, u32[]{:S(2)}) copy-start(bf16[8,24,256]{2,1,0:T(8,128)(2,1)} %param.15) | copy-start | bytes 294916
  337.3 17.1 %collective-permute-start.3 = (f32[64,2048]{1,0:T(8,128)}, f32[64,2048]{1,0:T(8,128)}, u32[]{:S(2)}, u32[]{:S(2)}) collective-permute-start(f32[64,2048]{1,0:T(8,128)} %reshape.151), channel_id=1, source_target_pairs={{16,0},{32,16},{48,32},{64,48},{80,64},{96,80},{112,96},{128,112},... | collective-permute-start | bytes 1572872 | tf_op jit(solution)/shard_map/ppermute | solution.py:64
  341.1 15.7 %collective-permute-start.2 = (f32[64,2048]{1,0:T(8,128)}, f32[64,2048]{1,0:T(8,128)}, u32[]{:S(2)}, u32[]{:S(2)}) collective-permute-start(f32[64,2048]{1,0:T(8,128)} %reshape.151), channel_id=1, source_target_pairs={{0,16},{16,32},{32,48},{48,64},{64,80},{80,96},{96,112},{112,128},... | collective-permute-start | bytes 1572872 | tf_op jit(solution)/shard_map/ppermute | solution.py:62
  401.2 0.8 copy-start.5
  441.8 0.8 copy-start.3
  454.7 20.5 %collective-permute-start.5 = (f32[64,2048]{1,0:T(8,128)}, f32[64,2048]{1,0:T(8,128)}, u32[]{:S(2)}, u32[]{:S(2)}) collective-permute-start(f32[64,2048]{1,0:T(8,128)} %copy.57), channel_id=1, source_target_pairs={{240,0},{0,16},{16,32},{32,48},{48,64},{64,80},{80,96},{96,112},{1... | collective-permute-start | bytes 1572872 | tf_op jit(solution)/shard_map/ppermute | solution.py:21
  463.1 14.3 %collective-permute-start.4 = (f32[64,2048]{1,0:T(8,128)}, f32[64,2048]{1,0:T(8,128)}, u32[]{:S(2)}, u32[]{:S(2)}) collective-permute-start(f32[64,2048]{1,0:T(8,128)} %copy.56), channel_id=1, source_target_pairs={{16,0},{32,16},{48,32},{64,48},{80,64},{96,80},{112,96},{128,112},... | collective-permute-start | bytes 1572872 | tf_op jit(solution)/shard_map/ppermute | solution.py:21
  574.9 16.0 %collective-permute-start.7 = (f32[64,2048]{1,0:T(8,128)}, f32[64,2048]{1,0:T(8,128)}, u32[]{:S(2)}, u32[]{:S(2)}) collective-permute-start(f32[64,2048]{1,0:T(8,128)} %reshape.155), channel_id=1, source_target_pairs={{16,0},{32,16},{48,32},{64,48},{80,64},{96,80},{112,96},{128,112},... | collective-permute-start | bytes 1572872 | tf_op jit(solution)/shard_map/ppermute | solution.py:64
  574.9 18.4 %collective-permute-start.6 = (f32[64,2048]{1,0:T(8,128)}, f32[64,2048]{1,0:T(8,128)}, u32[]{:S(2)}, u32[]{:S(2)}) collective-permute-start(f32[64,2048]{1,0:T(8,128)} %reshape.155), channel_id=1, source_target_pairs={{0,16},{16,32},{32,48},{48,64},{64,80},{80,96},{96,112},{112,128},... | collective-permute-start | bytes 1572872 | tf_op jit(solution)/shard_map/ppermute | solution.py:62
  635.6 0.8 copy-start.4
  677.7 0.8 copy-start.2
  690.7 20.2 %collective-permute-start.9 = (f32[64,2048]{1,0:T(8,128)}, f32[64,2048]{1,0:T(8,128)}, u32[]{:S(2)}, u32[]{:S(2)}) collective-permute-start(f32[64,2048]{1,0:T(8,128)} %copy.63), channel_id=1, source_target_pairs={{240,0},{0,16},{16,32},{32,48},{48,64},{64,80},{80,96},{96,112},{1... | collective-permute-start | bytes 1572872 | tf_op jit(solution)/shard_map/ppermute | solution.py:21
  698.8 14.6 %collective-permute-start.8 = (f32[64,2048]{1,0:T(8,128)}, f32[64,2048]{1,0:T(8,128)}, u32[]{:S(2)}, u32[]{:S(2)}) collective-permute-start(f32[64,2048]{1,0:T(8,128)} %copy.62), channel_id=1, source_target_pairs={{16,0},{32,16},{48,32},{64,48},{80,64},{96,80},{112,96},{128,112},... | collective-permute-start | bytes 1572872 | tf_op jit(solution)/shard_map/ppermute | solution.py:21
  809.0 16.0 %collective-permute-start.11 = (f32[64,2048]{1,0:T(8,128)}, f32[64,2048]{1,0:T(8,128)}, u32[]{:S(2)}, u32[]{:S(2)}) collective-permute-start(f32[64,2048]{1,0:T(8,128)} %reshape.159), channel_id=1, source_target_pairs={{16,0},{32,16},{48,32},{64,48},{80,64},{96,80},{112,96},{128,112},... | collective-permute-start | bytes 1572872 | tf_op jit(solution)/shard_map/ppermute | solution.py:64
  809.0 18.4 %collective-permute-start.10 = (f32[64,2048]{1,0:T(8,128)}, f32[64,2048]{1,0:T(8,128)}, u32[]{:S(2)}, u32[]{:S(2)}) collective-permute-start(f32[64,2048]{1,0:T(8,128)} %reshape.159), channel_id=1, source_target_pairs={{0,16},{16,32},{32,48},{48,64},{64,80},{80,96},{96,112},{112,128},... | collective-permute-start | bytes 1572872 | tf_op jit(solution)/shard_map/ppermute | solution.py:62
  871.4 40.1 %copy-start.7 = (f32[8,64,256]{2,1,0:T(8,128)}, f32[8,64,256]{2,1,0:T(8,128)S(1)}, u32[]{:S(2)}) copy-start(f32[8,64,256]{2,1,0:T(8,128)S(1)} %multiply_subtract_fusion) | copy-start | bytes 1572868
where the time goes:
time: 930 us; the launch traced here: 912 us
  blocking collectives  297 us (32%)
  other arithmetic  208 us (22%)
  matrix products  175 us (19%)
  local copies, waits for them, and re-layouts  133 us (14%)
  waiting for transfers between devices  57.6 us (6%)
  starting transfers between devices  39.3 us (4%)
    psum x30, blocking collectives, by_axis(): return functools.reduce(lax.psum, axes, x)  203 us
    another operation x4, other arithmetic, coarse_solve(): jax.scipy.linalg.solve_triangular(factor, forward, lower=True, trans=1)  169 us
    another operation x93, matrix products, coarse_solve(): jax.scipy.linalg.solve_triangular(factor, coarse_load.T, lower=True)  80 us
    another operation x93, matrix products, coarse_solve(): jax.scipy.linalg.solve_triangular(factor, forward, lower=True, trans=1)  74.5 us
    all_to_all x3, blocking collectives, sent_to_all(): lax.all_to_all(jnp.broadcast_to(x[None], (count, *x.shape)), axis, 0, 0,...  58.9 us
    another operation x85, local copies, waits for them, and re-layouts, coarse_solve(): jax.scipy.linalg.solve_triangular(factor, forward, lower=True, trans=1)  57.2 us
    all_to_all x2, blocking collectives, summed_on_arrival(): tiles = lax.all_to_all(cut_along(x, dim, count), axis, 0, 0, tiled=True)  35.5 us
    ppermute x3, waiting for transfers between devices, extended(): lax.ppermute(head, axis, [((i + 1) % count, i) for i in range(count)])  30.4 us
  transfers between devices with their start and end apart: 13, of which 8 were waited for; matrix products, arithmetic and copies ran while one was open for 27% of the time, Pallas kernels for 0%

commit v1 on v0

v1 whole, which is shorter than its diff:
```python
import functools

import jax
import jax.numpy as jnp
from jax import lax
from jax.experimental import pallas as pl
from jax.experimental.pallas import tpu as pltpu
from jax.sharding import PartitionSpec as P

ITERS = 3
MESH = pl.DeviceIdType.MESH
F32, BF16 = jnp.float32, jnp.bfloat16
BLK = 256


def nn(a, b):
    return lax.dot_general(a, b, (((1,), (0,)), ((), ())), preferred_element_type=F32)


def nt(a, b):
    return lax.dot_general(a, b, (((1,), (1,)), ((), ())), preferred_element_type=F32)


def pieces(x):
    high = x.astype(BF16)
    return high, (x - high.astype(F32)).astype(BF16)


def iota(shape, dim):
    return lax.broadcasted_iota(jnp.int32, shape, dim)


def kernel(
    n_grp, n_mem,
    r_in, d_in, kmat, dmat, cst, idx, factor,
    r_ref, d_ref, steps_ref,
    img, l_ref, xh, xl, oht, mask, a_ref,
    snd, rcv, snd2, rcv2, idx_all, load, nbr, ext, ar,
    fsem, sem_i, sem_f, sem_b, sem_n, sem_x, sem_a,
):
    subs, q_all, _ = r_in.shape
    nb = l_ref.shape[0] // BLK
    rows4 = 4 * nb
    n_rows = 3 * rows4
    me, grp = lax.axis_index("mem"), lax.axis_index("grp")
    top = iota((8, 128), 0) < 4
    top2 = iota((8, BLK), 0) < 4
    band = iota((q_all, 128), 1) // 32

    fetch = pltpu.make_async_copy(factor.at[0], l_ref, fsem)
    fetch.start()

    barrier = pltpu.get_barrier_semaphore()
    for step in range(1, n_mem):
        pl.semaphore_signal(
            barrier, inc=1, device_id={"mem": lax.rem(me + step, n_mem)}, device_id_type=MESH
        )
    for step in range(1, n_grp):
        pl.semaphore_signal(
            barrier, inc=1, device_id={"grp": lax.rem(grp + step, n_grp)}, device_id_type=MESH
        )
    pl.semaphore_wait(barrier, n_mem + n_grp - 2)

    def to_member(src, dst, sem, step):
        return pltpu.make_async_remote_copy(
            src_ref=src, dst_ref=dst, send_sem=sem.at[0, step], recv_sem=sem.at[1, step],
            device_id={"mem": lax.rem(me + step, n_mem)}, device_id_type=MESH,
        )

    def to_group(src, dst, sem, step):
        return pltpu.make_async_remote_copy(
            src_ref=src, dst_ref=dst, send_sem=sem.at[0, step], recv_sem=sem.at[1, step],
            device_id={"grp": lax.rem(grp + step, n_grp)}, device_id_type=MESH,
        )

    idx_all[pl.ds(me, 1)] = idx[...][None]
    for step in range(1, n_mem):
        to_member(idx, idx_all.at[me], sem_i, step).start()

    def reduce_start(which, row):
        mine = ar.at[which, 0]
        mine[pl.ds(me, 1)] = row[None]
        for step in range(1, n_mem):
            to_member(mine.at[me], mine.at[me], sem_a.at[which, 0], step).start()

    def reduce_middle(which):
        mine, other = ar.at[which, 0], ar.at[which, 1]
        for step in range(1, n_mem):
            to_member(mine.at[me], mine.at[lax.rem(me + n_mem - step, n_mem)], sem_a.at[which, 0], step).wait()
        row = jnp.sum(mine[...], axis=0)
        other[pl.ds(grp, 1)] = row[None]
        for step in range(1, n_grp):
            to_group(other.at[grp], other.at[grp], sem_a.at[which, 1], step).start()

    def reduce_end(which):
        other = ar.at[which, 1]
        for step in range(1, n_grp):
            to_group(other.at[grp], other.at[lax.rem(grp + n_grp - step, n_grp)], sem_a.at[which, 1], step).wait()
        return jnp.sum(other[...], axis=0)

    def all_reduce(which, row):
        reduce_start(which, row)
        reduce_middle(which)
        return reduce_end(which)

    def as_row(total):
        wide = jnp.concatenate([total, jnp.zeros((128 - q_all, BLK), F32)], axis=0)
        first, rest = wide.astype(BF16), wide
        ones = jnp.ones((8, BLK), BF16)
        rest = rest - first.astype(F32)
        second = rest.astype(BF16)
        third = (rest - second.astype(F32)).astype(BF16)
        out = nt(ones, first) + (nt(ones, second) + nt(ones, third))
        return out[0:1]

    def as_column(row):
        diagonal = iota((q_all, 128), 0) == iota((q_all, 128), 1)
        return jnp.sum(jnp.where(diagonal, jnp.broadcast_to(row, (q_all, 128)), 0.0), axis=1, keepdims=True)

    def halves_to_tiles(p0, p1):
        for v in range(q_all // 8):
            a, b = p0[8 * v : 8 * v + 8], p1[8 * v : 8 * v + 8]
            snd[2 * v] = jnp.where(top, a, pltpu.roll(b, 4, 0))
            snd[2 * v + 1] = jnp.where(top, pltpu.roll(a, 4, 0), b)

    def send_partials():
        halves = []
        for h in range(2):
            stack = []
            for s in range(4 * h, 4 * h + 4):
                stack += pieces(nn(d_ref[s].astype(BF16), kmat[s]))
            found = nt(jnp.concatenate(stack, axis=0), cst[h])
            total = jnp.zeros((q_all, 128), F32)
            for s in range(4):
                part = found[2 * s * q_all : (2 * s + 1) * q_all] + found[(2 * s + 1) * q_all : (2 * s + 2) * q_all]
                total = jnp.where(band == s, part, total)
            halves.append(total)
        halves_to_tiles(*halves)
        for step in range(1, n_mem):
            to_member(snd.at[lax.rem(me + step, n_mem)], rcv.at[me], sem_f, step).start()
        rcv[pl.ds(me, 1)] = snd[pl.ds(me, 1)]

    def invert_blocks():
        fetch.wait()
        row, col = iota((BLK, BLK), 0), iota((BLK, BLK), 1)

        def one(i, carry):
            at = pl.multiple_of(i * BLK, BLK)
            tri = l_ref[pl.ds(at, BLK), pl.ds(at, BLK)].astype(F32)
            inv = jnp.where(row == col, 1.0 / jnp.where(row == col, tri, 1.0), 0.0)
            size = 1
            while size < BLK:
                below = (row // (2 * size) == col // (2 * size)) & (row // size > col // size)
                off = jnp.where(below, tri, 0.0).astype(BF16)
                high, low = pieces(inv)
                left = nn(high, off) + nn(low, off)
                left_high, left_low = pieces(left)
                inv = inv - (nn(left_high, high) + (nn(left_high, low) + nn(left_low, high)))
                size *= 2
            high, low = pieces(inv)
            xh[pl.ds(i, 1)] = high[None]
            xl[pl.ds(i, 1)] = low[None]
            return carry

        lax.fori_loop(0, nb, one, 0)

    def build_masks():
        for step in range(1, n_mem):
            to_member(idx, idx_all.at[lax.rem(me + n_mem - step, n_mem)], sem_i, step).wait()

        def one(j, carry):
            tile = idx_all[pl.ds(j, 1)][0]
            for h in range(2):
                line = tile[4 * h : 4 * h + 1]
                at = pl.multiple_of(j * BLK + h * 128, 128)
                lo = jnp.broadcast_to(line & (BLK - 1), (BLK, 128))
                oht[:, pl.ds(at, 128)] = jnp.where(lo == iota((BLK, 128), 0), 1.0, 0.0).astype(BF16)
                hi = jnp.broadcast_to(line >> 8, (n_rows, 128))
                mask[:, pl.ds(at, 128)] = jnp.where(hi == iota((n_rows, 128), 0) // 4, 1.0, 0.0)
            return carry

        lax.fori_loop(0, n_mem, one, 0)

    def scatter():
        for step in range(n_mem):
            j = lax.rem(me + n_mem - step, n_mem)
            if step:
                to_member(snd.at[lax.rem(me + step, n_mem)], rcv.at[j], sem_f, step).wait()
            tile = rcv[pl.ds(j, 1)][0]
            high = tile.astype(BF16).astype(F32)
            for number, part in enumerate((high, tile - high)):
                turned = pltpu.roll(part, 4, 0)
                for h in range(2):
                    twice = jnp.where(top, part, turned) if h == 0 else jnp.where(top, turned, part)
                    at = pl.multiple_of(j * BLK + h * 128, 128)
                    full = jnp.concatenate([twice] * (n_rows // 8), axis=0) * mask[:, pl.ds(at, 128)]
                    a_ref[number * n_rows : (number + 1) * n_rows, pl.ds(at, 128)] = full.astype(BF16)
        both = nt(a_ref[...], oht[...])
        load[...] = both[:n_rows] + both[n_rows:]

    def fold_neighbours():
        up = to_group(load.at[2 * rows4 : 3 * rows4], nbr.at[0], sem_n, 1)
        down = to_group(load.at[0:rows4], nbr.at[1], sem_n, n_grp - 1)
        up.start()
        down.start()
        up.wait()
        down.wait()
        return load[rows4 : 2 * rows4] + nbr[0] + nbr[1]

    def twin(x):
        high, low = pieces(x)
        return jnp.where(top2, high.astype(F32), low.astype(F32)).astype(BF16)

    def folded(x):
        return x + pltpu.roll(x, 4, 0)

    def coarse_solve(b):
        acc = []
        for v in range(nb // 2):
            x = b[8 * v : 8 * v + 8]
            y = pltpu.roll(x, 4, 0)
            acc += [jnp.where(top2, x, y), jnp.where(top2, y, x)]
        for i in range(nb):
            p = twin(acc[i])
            acc[i] = folded(nt(p, xh[i]) + nt(p, xl[i]))
            p = twin(acc[i])
            for t in range(i + 1, nb):
                acc[t] = acc[t] - folded(nt(p, l_ref[t * BLK : (t + 1) * BLK, i * BLK : (i + 1) * BLK]))
        for i in reversed(range(nb)):
            p = twin(acc[i])
            acc[i] = folded(nn(p, xh[i]) + nn(p, xl[i]))
            p = twin(acc[i])
            for t in range(i):
                acc[t] = acc[t] - folded(nn(p, l_ref[i * BLK : (i + 1) * BLK, t * BLK : (t + 1) * BLK]))
        for v in range(nb // 2):
            ext[rows4 + 8 * v : rows4 + 8 * v + 8] = jnp.where(top2, acc[2 * v], acc[2 * v + 1])

    def spread_neighbours():
        own = ext.at[rows4 : 2 * rows4]
        up = to_group(own, ext.at[0:rows4], sem_x, 1)
        down = to_group(own, ext.at[2 * rows4 : 3 * rows4], sem_x, n_grp - 1)
        up.start()
        down.start()
        up.wait()
        down.wait()

    def pick():
        high, low = pieces(ext[...])
        both = jnp.concatenate([high, low], axis=0)
        for step in list(range(1, n_mem)) + [0]:
            j = lax.rem(me + step, n_mem)
            at = pl.multiple_of(j * BLK, BLK)
            found = nn(both, oht[:, pl.ds(at, BLK)])
            found = (found[:n_rows] + found[n_rows:]) * mask[:, pl.ds(at, BLK)]
            total = found[0:8]
            for v in range(1, n_rows // 8):
                total = total + found[8 * v : 8 * v + 8]
            total = folded(total)
            tile = jnp.where(top, total[:, :128], total[:, 128:])
            if step:
                snd2[pl.ds(j, 1)] = tile[None]
                to_member(snd2.at[j], rcv2.at[me], sem_b, step).start()
            else:
                rcv2[pl.ds(me, 1)] = tile[None]
        for step in range(1, n_mem):
            to_member(
                snd2.at[lax.rem(me + step, n_mem)], rcv2.at[lax.rem(me + n_mem - step, n_mem)], sem_b, step
            ).wait()
        halves = ([], [])
        for v in range(q_all // 8):
            a, b = rcv2[2 * v], rcv2[2 * v + 1]
            halves[0].append(jnp.where(top, a, pltpu.roll(b, 4, 0)))
            halves[1].append(jnp.where(top, pltpu.roll(a, 4, 0), b))
        return [jnp.concatenate(half, axis=0) for half in halves]

    def make_image(halves):
        total = jnp.zeros((q_all, BLK), F32)
        for h in range(2):
            stack = []
            for s in range(4):
                stack += pieces(jnp.where(band == s, halves[h], 0.0))
            found = nn(jnp.concatenate(stack, axis=0), cst[h])
            for s in range(4):
                lifted = found[2 * s * q_all : (2 * s + 1) * q_all] + found[(2 * s + 1) * q_all : (2 * s + 2) * q_all]
                direction = d_ref[4 * h + s]
                image = nn((direction + lifted).astype(BF16), kmat[4 * h + s])
                img[4 * h + s] = image
                total = total + direction * image
        return total

    r_ref[...] = r_in[...]
    d_ref[...] = d_in[...]
    total = jnp.zeros((q_all, BLK), F32)
    for s in range(subs):
        total = total + r_ref[s] * nn(r_ref[s].astype(BF16), dmat[s])
    reduce_start(0, as_row(total))
    send_partials()
    reduce_middle(0)
    build_masks()
    invert_blocks()
    norm_start = reduce_end(0)

    def iteration(t, norm_now):
        scatter()
        coarse_solve(fold_neighbours())
        spread_neighbours()
        total = make_image(pick())
        curvature = all_reduce(1, as_row(total))
        alpha = norm_now / curvature
        steps_ref[pl.ds(t, 1), :] = alpha
        column = as_column(alpha)
        total = jnp.zeros((q_all, BLK), F32)
        for s in range(subs):
            residual = r_ref[s] - column * img[s]
            r_ref[s] = residual
            precond = nn(residual.astype(BF16), dmat[s])
            img[s] = precond
            total = total + residual * precond
        norm_next = all_reduce(0, as_row(total))
        column = as_column(norm_next / norm_now)
        for s in range(subs):
            d_ref[s] = img[s] + column * d_ref[s]

        @pl.when(t < ITERS - 1)
        def _():
            send_partials()

        return norm_next

    lax.fori_loop(0, ITERS, iteration, norm_start)


def local(n_grp, n_mem, residual, direction, local_inverse, dirichlet, coupling, corner_map, coarse_factor):
    subs, q_all, nr = residual.shape
    corners = coupling.shape[1]
    order = coarse_factor.shape[1]
    nb = order // BLK
    n_rows = 12 * nb
    cst = jnp.pad(coupling, ((0, 0), (0, 32 - corners), (0, 0))).reshape(2, 128, nr)
    idx = jnp.pad(corner_map, ((0, 0), (0, 32 - corners)), constant_values=-1).reshape(2, 1, 128)
    idx = jnp.broadcast_to(idx, (2, 4, 128)).reshape(8, 128)
    vmem = pl.BlockSpec(memory_space=pltpu.VMEM)
    dma = pltpu.SemaphoreType.DMA
    residual, direction, steps = pl.pallas_call(
        functools.partial(kernel, n_grp, n_mem),
        out_shape=(
            jax.ShapeDtypeStruct(residual.shape, F32),
            jax.ShapeDtypeStruct(residual.shape, F32),
            jax.ShapeDtypeStruct((8, 128), F32),
        ),
        in_specs=[vmem] * 6 + [pl.BlockSpec(memory_space=pl.ANY)],
        out_specs=(vmem,) * 3,
        scratch_shapes=[
            pltpu.VMEM((subs, q_all, nr), F32),
            pltpu.VMEM((order, order), BF16),
            pltpu.VMEM((nb, BLK, BLK), BF16),
            pltpu.VMEM((nb, BLK, BLK), BF16),
            pltpu.VMEM((BLK, n_mem * BLK), BF16),
            pltpu.VMEM((n_rows, n_mem * BLK), F32),
            pltpu.VMEM((2 * n_rows, n_mem * BLK), BF16),
            pltpu.VMEM((n_mem, 8, 128), F32),
            pltpu.VMEM((n_mem, 8, 128), F32),
            pltpu.VMEM((n_mem, 8, 128), F32),
            pltpu.VMEM((n_mem, 8, 128), F32),
            pltpu.VMEM((n_mem, 8, 128), jnp.int32),
            pltpu.VMEM((n_rows, BLK), F32),
            pltpu.VMEM((2, 4 * nb, BLK), F32),
            pltpu.VMEM((n_rows, BLK), F32),
            pltpu.VMEM((2, 2, max(n_mem, n_grp), 1, 128), F32),
            dma,
            dma((2, n_mem)),
            dma((2, n_mem)),
            dma((2, n_mem)),
            dma((2, n_grp)),
            dma((2, n_grp)),
            dma((2, 2, 2, max(n_mem, n_grp))),
        ],
        compiler_params=pltpu.CompilerParams(
            collective_id=0, has_side_effects=True, vmem_limit_bytes=64 * 1024 * 1024 - 512 * 1024
        ),
    )(residual, direction, local_inverse, dirichlet, cst, idx, coarse_factor)
    return residual, direction, steps[:ITERS, :q_all]


def solution(mesh):
    both = ("grp", "mem")
    return jax.shard_map(
        functools.partial(local, mesh.shape["grp"], mesh.shape["mem"]),
        mesh=mesh,
        in_specs=(P(both), P(both), P(both), P(both), P(both), P(both), P("grp")),
        out_specs=(P(both), P(both), P()),
        check_vma=False,
    )
```

time: 930 us -> 204 us (0.22); the launches traced: 912 us -> 203 us
  blocking collectives: 297 us -> 0 us
  other arithmetic: 208 us -> 0 us
  Pallas kernels: 0 us -> 195 us
  matrix products: 175 us -> 0 us
  local copies, waits for them, and re-layouts: 133 us -> 7.92 us
  waiting for transfers between devices: 57.6 us -> 0 us
  starting transfers between devices: 39.3 us -> 0 us
    psum x30 -> x0, blocking collectives: 203 us -> none  [by_axis(): return functools.reduce(lax.psum, axes, x)]
    pallas_call x0 -> x1, Pallas kernels: none -> 195 us  [local(): pl.pallas_call(functools.partial(kernel, n_grp, n_mem), out_shape=(jax.Sh...]
    another operation x5 -> x0, other arithmetic: 170 us -> none  [the longest x4 169 us: coarse_solve(): jax.scipy.linalg.solve_triangular(factor, forward, lower=True, trans=1)]
    another operation x186 -> x0, matrix products: 155 us -> none  [the longest x93 80 us: coarse_solve(): jax.scipy.linalg.solve_triangular(factor, coarse_load.T, lower=True)]
    all_to_all x5 -> x0, blocking collectives: 94.3 us -> none  [the longest x3 58.9 us: sent_to_all(): lax.all_to_all(jnp.broadcast_to(x[None], (count, *x.shape)), axis, 0, 0,...]
    ppermute x12 -> x0, waiting for transfers between devices: 57.6 us -> none  [the longest x3 30.4 us: extended(): lax.ppermute(head, axis, [((i + 1) % count, i) for i in range(count)])]
    another operation x85 -> x0, local copies, waits for them, and re-layouts: 57.2 us -> none  [coarse_solve(): jax.scipy.linalg.solve_triangular(factor, forward, lower=True, trans=1)]
    ppermute x12 -> x0, starting transfers between devices: 31.6 us -> none  [the longest x6 20.8 us: from_behind(): return lax.ppermute(block, axis, route)]
  transfers between devices with their start and end apart: 13 -> 0, of which waited for: 8 -> 0; matrix products, arithmetic and copies ran while one was open for 27% -> 0% of each run, Pallas kernels for 0% -> 0%
where the time goes in v1:
time: 204 us; the launch traced here: 203 us
  Pallas kernels  195 us (96%)
  local copies, waits for them, and re-layouts  7.92 us (4%)
    pallas_call x1, Pallas kernels, local(): pl.pallas_call(functools.partial(kernel, n_grp, n_mem), out_shape=(jax.Sh...  195 us

profile of v1, /device:TPU:1, one launch (start us, length us, event | category | flops | bytes accessed | tf_op | source)
XLA Modules:
  0.0 203.3 jit_solution(9800080297549465724)
XLA Ops:
  0.6 0.7 pad.9
  1.3 0.1 broadcast_in_dim.7
  1.4 0.6 broadcast_in_dim.8
  2.0 1.6 pad.8
  3.6 194.8 %shard_map.94 = (f32[8,64,256]{2,1,0:T(8,128)}, f32[8,64,256]{2,1,0:T(8,128)}, f32[8,128]{1,0:T(8,128)}) custom-call(f32[8,64,256]{2,1,0:T(8,128)} %r_in.1, f32[8,64,256]{2,1,0:T(8,128)} %d_in.1, bf16[8,256,256]{2,1,0:T(8,128)(2,1)} %kmat.1, bf16[8,256,256]{2,1,0:T(8,128)(2,1)} %dmat.1, bf16[2,128,256]{2,1,0:T(8,128)(2,1)} %bitcast.2, s32[8,128]{1,0:T(8,128)} %bitcast.3, ...), custom_call_target="tpu_custom_call" | custom-call | tf_op jit(solution)/shard_map/pallas_call | solution.py:344
  198.3 1.3 slice.3
  199.6 1.9 copy.12
  201.5 1.9 copy.13

commit v2 on v1

v2 whole, which is shorter than its diff:
```python
import functools

import jax
import jax.numpy as jnp
from jax import lax
from jax.experimental import pallas as pl
from jax.experimental.pallas import tpu as pltpu
from jax.sharding import PartitionSpec as P

ITERS = 3
MESH = pl.DeviceIdType.MESH
F32, BF16 = jnp.float32, jnp.bfloat16
BLK = 256


def nn(a, b):
    return lax.dot_general(a, b, (((1,), (0,)), ((), ())), preferred_element_type=F32)


def nt(a, b):
    return lax.dot_general(a, b, (((1,), (1,)), ((), ())), preferred_element_type=F32)


def pieces(x):
    high = x.astype(BF16)
    return high, (x - high.astype(F32)).astype(BF16)


def iota(shape, dim):
    return lax.broadcasted_iota(jnp.int32, shape, dim)


def kernel(
    n_grp, n_mem,
    r_in, d_in, kmat_in, dmat_in, coupling_in, corner_map, factor,
    r_ref, d_ref, steps_ref,
    kmat, dmat, coupling, cst, v_ref, solved, track, lift, l_ref, xh, xl, oht, mask, a_ref,
    idx, snd, rcv, snd2, rcv2, idx_all, load, nbr, ext, y_ref, ar,
    sem_l, sem_i, sem_f, sem_b, sem_n, sem_x, sem_a,
):
    subs, q_all, _ = r_in.shape
    corners = coupling_in.shape[1]
    nb = l_ref.shape[0] // BLK
    rows4 = 4 * nb
    n_rows = 3 * rows4
    me, grp = lax.axis_index("mem"), lax.axis_index("grp")
    top = iota((8, 128), 0) < 4
    top2 = iota((8, BLK), 0) < 4
    band = iota((q_all, 128), 1) // 32
    order = [0]
    for near in range(1, n_mem // 2):
        order += [near, n_mem - near]
    order.append(n_mem // 2)
    chunk = min(4, n_mem)

    barrier = pltpu.get_barrier_semaphore()
    for step in range(1, n_mem):
        pl.semaphore_signal(
            barrier, inc=1, device_id={"mem": lax.rem(me + step, n_mem)}, device_id_type=MESH
        )
    for step in range(1, n_grp):
        pl.semaphore_signal(
            barrier, inc=1, device_id={"grp": lax.rem(grp + step, n_grp)}, device_id_type=MESH
        )

    fetches = [
        pltpu.make_async_copy(src, dst, sem_l.at[number])
        for number, (src, dst) in enumerate(
            ((d_in, v_ref), (kmat_in, kmat), (coupling_in, coupling), (r_in, r_ref), (dmat_in, dmat), (factor.at[0], l_ref))
        )
    ]
    for fetch in fetches:
        fetch.start()

    def to_member(src, dst, sem, step):
        return pltpu.make_async_remote_copy(
            src_ref=src, dst_ref=dst, send_sem=sem.at[0, step], recv_sem=sem.at[1, step],
            device_id={"mem": lax.rem(me + step, n_mem)}, device_id_type=MESH,
        )

    def to_group(src, dst, sem, step):
        return pltpu.make_async_remote_copy(
            src_ref=src, dst_ref=dst, send_sem=sem.at[0, step], recv_sem=sem.at[1, step],
            device_id={"grp": lax.rem(grp + step, n_grp)}, device_id_type=MESH,
        )

    def member_at(step):
        return lax.rem(me + step, n_mem)

    def reduce_start(which, row):
        mine = ar.at[which, 0]
        mine[pl.ds(me, 1)] = row[None]
        for step in reversed(order[1:]):
            to_member(mine.at[me], mine.at[me], sem_a.at[which, 0], step).start()

    def reduce_middle(which):
        mine, other = ar.at[which, 0], ar.at[which, 1]
        for step in range(1, n_mem):
            to_member(mine.at[me], mine.at[member_at(n_mem - step)], sem_a.at[which, 0], step).wait()
        row = jnp.sum(mine[0:n_mem], axis=0)
        other[pl.ds(grp, 1)] = row[None]
        for step in range(1, n_grp):
            to_group(other.at[grp], other.at[grp], sem_a.at[which, 1], step).start()

    def reduce_end(which):
        other = ar.at[which, 1]
        for step in range(1, n_grp):
            to_group(other.at[grp], other.at[lax.rem(grp + n_grp - step, n_grp)], sem_a.at[which, 1], step).wait()
        return jnp.sum(other[0:n_grp], axis=0)

    def as_row(total):
        wide = jnp.concatenate([total, jnp.zeros((128 - q_all, BLK), F32)], axis=0)
        first, rest = wide.astype(BF16), wide
        ones = jnp.ones((8, BLK), BF16)
        rest = rest - first.astype(F32)
        second = rest.astype(BF16)
        third = (rest - second.astype(F32)).astype(BF16)
        out = nt(ones, first) + (nt(ones, second) + nt(ones, third))
        return out[0:1]

    def as_column(row):
        diagonal = iota((q_all, 128), 0) == iota((q_all, 128), 1)
        return jnp.sum(jnp.where(diagonal, jnp.broadcast_to(row, (q_all, 128)), 0.0), axis=1, keepdims=True)

    mine4 = iota((8, 128), 1) == 4 * me + lax.rem(iota((8, 128), 0), 4)

    def as_my_column(row):
        return jnp.sum(jnp.where(mine4, jnp.broadcast_to(row, (8, 128)), 0.0), axis=1, keepdims=True)

    def as_my_row(column):
        return jnp.sum(jnp.where(mine4 & top, jnp.broadcast_to(column, (8, 128)), 0.0), axis=0, keepdims=True)

    def build_tables():
        cst[...] = jnp.zeros(cst.shape, BF16)
        for s in range(subs):
            cst[s // 4, 32 * (s % 4) : 32 * (s % 4) + corners, :] = coupling[s]
        idx[...] = jnp.full((8, 128), -1, jnp.int32)
        idx[:, 0:corners] = corner_map[...]
        wide = idx[...]
        lane, sub = iota((8, 128), 1) // 32, iota((8, 128), 0)
        tile = jnp.full((8, 128), -1, jnp.int32)
        for s in range(subs):
            turned = pltpu.roll(wide, 32 * (s % 4), 1)[s : s + 1] if s % 4 else wide[s : s + 1]
            tile = jnp.where((lane == s % 4) & (sub // 4 == s // 4), jnp.broadcast_to(turned, (8, 128)), tile)
        idx[...] = tile

    def local_partials():
        halves = []
        for h in range(2):
            stack = []
            for s in range(4 * h, 4 * h + 4):
                out = nn(v_ref[s].astype(BF16), kmat[s])
                solved[s] = out
                stack += pieces(out)
            found = nt(jnp.concatenate(stack, axis=0), cst[h])
            total = jnp.zeros((q_all, 128), F32)
            for s in range(4):
                part = found[2 * s * q_all : (2 * s + 1) * q_all] + found[(2 * s + 1) * q_all : (2 * s + 2) * q_all]
                total = jnp.where(band == s, part, total)
            halves.append(total)
        for v in range(q_all // 8):
            a, b = halves[0][8 * v : 8 * v + 8], halves[1][8 * v : 8 * v + 8]
            snd[2 * v] = jnp.where(top, a, pltpu.roll(b, 4, 0))
            snd[2 * v + 1] = jnp.where(top, pltpu.roll(a, 4, 0), b)

    def send_partials():
        for step in reversed(order[1:]):
            to_member(snd.at[member_at(step)], rcv.at[me], sem_f, step).start()
        rcv[pl.ds(me, 1)] = snd[pl.ds(me, 1)]

    def block(i, j):
        return l_ref[i * BLK : (i + 1) * BLK, j * BLK : (j + 1) * BLK]

    def triple(left, high, low):
        left_high, left_low = pieces(left)
        return nn(left_high, high) + (nn(left_high, low) + nn(left_low, high))

    def invert_blocks(first, count):
        row, col = iota((BLK, BLK), 0), iota((BLK, BLK), 1)
        inverses = []
        for i in range(first, first + count):
            tri = block(i, i).astype(F32)
            diag = jnp.where(row == col, tri, 0.0)
            down = 1.0 / jnp.sum(diag, axis=1, keepdims=True)
            across = 1.0 / jnp.sum(diag, axis=0, keepdims=True)
            below = (row // 2 == col // 2) & (row > col)
            inverses.append(jnp.where(row == col, down, 0.0) - jnp.where(below, tri * down * across, 0.0))
        size = 2
        while size < BLK // 2:
            below = (row // (2 * size) == col // (2 * size)) & (row // size > col // size)
            split = [pieces(inv) for inv in inverses]
            lefts = []
            for number, (high, low) in enumerate(split):
                off = jnp.where(below, block(first + number, first + number).astype(F32), 0.0).astype(BF16)
                lefts.append(nn(high, off) + nn(low, off))
            inverses = [inv - triple(left, *pair) for inv, left, pair in zip(inverses, lefts, split)]
            size *= 2
        half = BLK // 2
        for number, inv in enumerate(inverses):
            i = first + number
            high, low = pieces(inv)
            xh[i // 2, i % 2] = high
            xl[i // 2, i % 2] = low
            off = l_ref[i * BLK + half : (i + 1) * BLK, i * BLK : i * BLK + half]
            left = nn(high[half:, half:], off) + nn(low[half:, half:], off)
            high, low = pieces(-triple(left, high[:half, :half], low[:half, :half]))
            xh[i // 2, i % 2, half:, :half] = high
            xl[i // 2, i % 2, half:, :half] = low
        for u in range(first // 2, (first + count) // 2):
            off = block(2 * u + 1, 2 * u)
            left = nn(xh[u, 1], off) + nn(xl[u, 1], off)
            xh[u, 2], xl[u, 2] = pieces(-triple(left, xh[u, 0], xl[u, 0]))

    def build_masks():
        for step in range(1, n_mem):
            to_member(idx, idx_all.at[member_at(n_mem - step)], sem_i, step).wait()
        for position, step in enumerate(order):
            tile = idx_all[pl.ds(member_at(n_mem - step), 1)][0]
            for h in range(2):
                line = tile[4 * h : 4 * h + 1]
                at = position * BLK + h * 128
                lo = jnp.broadcast_to(line & (BLK - 1), (BLK, 128))
                oht[:, at : at + 128] = jnp.where(lo == iota((BLK, 128), 0), 1.0, 0.0).astype(BF16)
                hi = jnp.broadcast_to(line >> 8, (n_rows, 128))
                mask[:, at : at + 128] = jnp.where(hi == iota((n_rows, 128), 0) // 4, 1.0, 0.0)

    def scatter():
        total = jnp.zeros((2 * n_rows, BLK), F32)
        for position, step in enumerate(order):
            j = member_at(n_mem - step)
            if step:
                to_member(snd.at[member_at(step)], rcv.at[j], sem_f, step).wait()
            tile = rcv[pl.ds(j, 1)][0]
            high = tile.astype(BF16).astype(F32)
            for number, part in enumerate((high, tile - high)):
                turned = pltpu.roll(part, 4, 0)
                for h in range(2):
                    twice = jnp.where(top, part, turned) if h == 0 else jnp.where(top, turned, part)
                    at = position * BLK + h * 128
                    full = jnp.concatenate([twice] * (n_rows // 8), axis=0) * mask[:, at : at + 128]
                    a_ref[number * n_rows : (number + 1) * n_rows, at : at + 128] = full.astype(BF16)
            if position % chunk == chunk - 1:
                at = slice((position + 1 - chunk) * BLK, (position + 1) * BLK)
                total = total + nt(a_ref[:, at], oht[:, at])
        load[...] = total[:n_rows] + total[n_rows:]

    def twin(x):
        high, low = pieces(x)
        return jnp.where(top2, high.astype(F32), low.astype(F32)).astype(BF16)

    def folded(x):
        return x + pltpu.roll(x, 4, 0)

    def lower(b):
        acc = []
        for v in range(nb // 2):
            x = b[8 * v : 8 * v + 8]
            y = pltpu.roll(x, 4, 0)
            acc += [jnp.where(top2, x, y), jnp.where(top2, y, x)]
        for u in range(nb // 2):
            p0, p1 = twin(acc[2 * u]), twin(acc[2 * u + 1])
            y0 = nt(p0, xh[u, 0]) + nt(p0, xl[u, 0])
            y1 = (nt(p0, xh[u, 2]) + nt(p0, xl[u, 2])) + (nt(p1, xh[u, 1]) + nt(p1, xl[u, 1]))
            acc[2 * u], acc[2 * u + 1] = folded(y0), folded(y1)
            p0, p1 = twin(acc[2 * u]), twin(acc[2 * u + 1])
            for t in range(2 * u + 2, nb):
                acc[t] = acc[t] - folded(nt(p0, block(t, 2 * u)) + nt(p1, block(t, 2 * u + 1)))
        return acc

    def upper(acc):
        for u in reversed(range(nb // 2)):
            p0, p1 = twin(acc[2 * u]), twin(acc[2 * u + 1])
            x1 = nn(p1, xh[u, 1]) + nn(p1, xl[u, 1])
            x0 = (nn(p0, xh[u, 0]) + nn(p0, xl[u, 0])) + (nn(p1, xh[u, 2]) + nn(p1, xl[u, 2]))
            acc[2 * u], acc[2 * u + 1] = folded(x0), folded(x1)
            p0, p1 = twin(acc[2 * u]), twin(acc[2 * u + 1])
            for t in range(2 * u):
                acc[t] = acc[t] - folded(nn(p0, block(2 * u, t)) + nn(p1, block(2 * u + 1, t)))
        for v in range(nb // 2):
            ext[rows4 + 8 * v : rows4 + 8 * v + 8] = jnp.where(top2, acc[2 * v], acc[2 * v + 1])

    def pick():
        high, low = pieces(ext[...])
        both = jnp.concatenate([high, low], axis=0)
        for position in reversed(range(n_mem)):
            step = (n_mem - order[position]) % n_mem
            j = member_at(step)
            at = slice(position * BLK, (position + 1) * BLK)
            found = nn(both, oht[:, at])
            found = (found[:n_rows] + found[n_rows:]) * mask[:, at]
            total = found[0:8]
            for v in range(1, n_rows // 8):
                total = total + found[8 * v : 8 * v + 8]
            total = folded(total)
            tile = jnp.where(top, total[:, :128], total[:, 128:])
            if step:
                snd2[pl.ds(j, 1)] = tile[None]
                to_member(snd2.at[j], rcv2.at[me], sem_b, step).start()
            else:
                rcv2[pl.ds(me, 1)] = tile[None]

    def picked():
        for step in order[1:]:
            to_member(snd2.at[member_at(step)], rcv2.at[member_at(n_mem - step)], sem_b, step).wait()
        halves = ([], [])
        for v in range(q_all // 8):
            a, b = rcv2[2 * v], rcv2[2 * v + 1]
            halves[0].append(jnp.where(top, a, pltpu.roll(b, 4, 0)))
            halves[1].append(jnp.where(top, pltpu.roll(a, 4, 0), b))
        return [jnp.concatenate(half, axis=0) for half in halves]

    def update(halves, alpha, beta):
        total = jnp.zeros((q_all, BLK), F32)
        for h in range(2):
            stack = []
            for s in range(4):
                stack += pieces(jnp.where(band == s, halves[h], 0.0))
            found = nn(jnp.concatenate(stack, axis=0), cst[h])
            for s in range(4):
                lifted = found[2 * s * q_all : (2 * s + 1) * q_all] + found[(2 * s + 1) * q_all : (2 * s + 2) * q_all]
                at = 4 * h + s
                lifted = lifted + beta * lift[at]
                lift[at] = lifted
                image = nn((d_ref[at] + lifted).astype(BF16), kmat[at])
                residual = r_ref[at] - alpha * image
                r_ref[at] = residual
                precond = nn(residual.astype(BF16), dmat[at])
                v_ref[at] = precond
                total = total + residual * precond
        return total

    d_ref[...] = jnp.zeros(d_ref.shape, F32)
    track[...] = jnp.zeros(track.shape, F32)
    lift[...] = jnp.zeros(lift.shape, F32)
    y_ref[...] = jnp.zeros(y_ref.shape, F32)
    for fetch in fetches[:3]:
        fetch.wait()
    build_tables()
    local_partials()
    for fetch in fetches[3:5]:
        fetch.wait()
    total = jnp.zeros((q_all, BLK), F32)
    for s in range(subs):
        total = total + r_ref[s] * nn(r_ref[s].astype(BF16), dmat[s])
    first_row = as_row(total)
    pl.semaphore_wait(barrier, n_mem + n_grp - 2)
    reduce_start(0, first_row)
    send_partials()
    idx_all[pl.ds(me, 1)] = idx[...][None]
    for step in reversed(order[1:]):
        to_member(idx, idx_all.at[me], sem_i, step).start()
    fetches[5].wait()
    group = min(4, nb)
    invert_blocks(0, group)
    build_masks()
    for start in range(group, nb, group):
        invert_blocks(start, group)

    def iteration(t, norm_before):
        reduce_middle(0)
        scatter()
        up = to_group(load.at[2 * rows4 : 3 * rows4], nbr.at[0], sem_n, 1)
        down = to_group(load.at[0:rows4], nbr.at[1], sem_n, n_grp - 1)
        up.start()
        down.start()
        norm_now = reduce_end(0)
        beta = jnp.where(t == 0, 0.0, norm_now / norm_before)
        beta_column = as_column(beta)
        total = jnp.zeros((q_all, BLK), F32)
        for s in range(subs):
            direction = v_ref[s] + beta_column * d_ref[s]
            d_ref[s] = direction
            follow = solved[s] + beta_column * track[s]
            track[s] = follow
            total = total + direction * follow
        local_row = as_row(total)
        up.wait()
        down.wait()
        acc = lower(load[rows4 : 2 * rows4] + nbr[0] + nbr[1])
        my_beta = as_my_column(beta)
        squares = jnp.zeros((8, BLK), F32)
        for i in range(nb):
            y = acc[i] + my_beta * y_ref[i]
            y_ref[i] = y
            squares = squares + y * y
        reduce_start(1, local_row + as_my_row(jnp.sum(squares, axis=1, keepdims=True)))
        upper(acc)
        own = ext.at[rows4 : 2 * rows4]
        up = to_group(own, ext.at[0:rows4], sem_x, 1)
        down = to_group(own, ext.at[2 * rows4 : 3 * rows4], sem_x, n_grp - 1)
        up.start()
        down.start()
        reduce_middle(1)
        up.wait()
        down.wait()
        pick()
        alpha = norm_now / reduce_end(1)
        steps_ref[pl.ds(t, 1), :] = alpha[:, :q_all]
        reduce_start(0, as_row(update(picked(), as_column(alpha), beta_column)))

        @pl.when(t < ITERS - 1)
        def _():
            local_partials()
            send_partials()

        return norm_now

    norm_before = lax.fori_loop(0, ITERS, iteration, jnp.ones((1, 128), F32))
    reduce_middle(0)
    beta_column = as_column(reduce_end(0) / norm_before)
    for s in range(subs):
        d_ref[s] = v_ref[s] + beta_column * d_ref[s]


def local(n_grp, n_mem, residual, direction, local_inverse, dirichlet, coupling, corner_map, coarse_factor):
    subs, q_all, nr = residual.shape
    order = coarse_factor.shape[1]
    nb = order // BLK
    n_rows = 12 * nb
    most = max(n_mem, n_grp)
    dma = pltpu.SemaphoreType.DMA
    vmem = pl.BlockSpec(memory_space=pltpu.VMEM)
    anywhere = pl.BlockSpec(memory_space=pl.ANY)
    field = pltpu.VMEM(residual.shape, F32)
    tiles = pltpu.VMEM((n_mem, 8, 128), F32)
    return pl.pallas_call(
        functools.partial(kernel, n_grp, n_mem),
        out_shape=(
            jax.ShapeDtypeStruct(residual.shape, F32),
            jax.ShapeDtypeStruct(residual.shape, F32),
            jax.ShapeDtypeStruct((ITERS, q_all), F32),
        ),
        in_specs=[anywhere] * 5 + [vmem, anywhere],
        out_specs=(vmem,) * 3,
        scratch_shapes=[
            pltpu.VMEM(local_inverse.shape, BF16),
            pltpu.VMEM(dirichlet.shape, BF16),
            pltpu.VMEM(coupling.shape, BF16),
            pltpu.VMEM((2, 128, nr), BF16),
            field,
            field,
            field,
            field,
            pltpu.VMEM((order, order), BF16),
            pltpu.VMEM((nb // 2, 3, BLK, BLK), BF16),
            pltpu.VMEM((nb // 2, 3, BLK, BLK), BF16),
            pltpu.VMEM((BLK, n_mem * BLK), BF16),
            pltpu.VMEM((n_rows, n_mem * BLK), F32),
            pltpu.VMEM((2 * n_rows, n_mem * BLK), BF16),
            pltpu.VMEM((8, 128), jnp.int32),
            tiles,
            tiles,
            tiles,
            tiles,
            pltpu.VMEM((n_mem, 8, 128), jnp.int32),
            pltpu.VMEM((n_rows, BLK), F32),
            pltpu.VMEM((2, 4 * nb, BLK), F32),
            pltpu.VMEM((n_rows, BLK), F32),
            pltpu.VMEM((nb, 8, BLK), F32),
            pltpu.VMEM((2, 2, most, 1, 128), F32),
            dma((6,)),
            dma((2, n_mem)),
            dma((2, n_mem)),
            dma((2, n_mem)),
            dma((2, n_grp)),
            dma((2, n_grp)),
            dma((2, 2, 2, most)),
        ],
        compiler_params=pltpu.CompilerParams(
            collective_id=0, has_side_effects=True, vmem_limit_bytes=63 * 1024 * 1024
        ),
    )(residual, direction, local_inverse, dirichlet, coupling, corner_map, coarse_factor)


def solution(mesh):
    both = ("grp", "mem")
    return jax.shard_map(
        functools.partial(local, mesh.shape["grp"], mesh.shape["mem"]),
        mesh=mesh,
        in_specs=(P(both), P(both), P(both), P(both), P(both), P(both), P("grp")),
        out_specs=(P(both), P(both), P()),
        check_vma=False,
    )
```

time: 204 us -> 119 us (0.58)
  Pallas kernels: 195 us -> 113 us
  local copies, waits for them, and re-layouts: 7.92 us -> 4.99 us
    pallas_call x1, Pallas kernels: 195 us -> 113 us  [local(): pl.pallas_call(functools.partial(kernel, n_grp, n_mem), out_shape=(jax.Sh...]
    pad x2 -> x0, local copies, waits for them, and re-layouts: 2.25 us -> none  [the longest x1 1.56 us: local(): jnp.pad(coupling, ((0, 0), (0, 32 - corners), (0, 0))).reshape(2, 128, nr)]
    unnamed x2 -> x3, local copies, waits for them, and re-layouts: 3.73 us -> 4.99 us
where the time goes in v2:
time: 119 us
  Pallas kernels  113 us (95%)
  local copies, waits for them, and re-layouts  4.99 us (4%)
    pallas_call x1, Pallas kernels, local(): pl.pallas_call(functools.partial(kernel, n_grp, n_mem), out_shape=(jax.Sh...  113 us
    unnamed x3, local copies, waits for them, and re-layouts  4.99 us

profile of v2, /device:TPU:1, one launch (start us, length us, event | category | flops | bytes accessed | tf_op | source)
XLA Modules:
  0.0 119.1 jit_solution(16176383633970828728)
XLA Ops:
  0.6 113.4 %shard_map.94 = (f32[8,64,256]{2,1,0:T(8,128)}, f32[8,64,256]{2,1,0:T(8,128)}, f32[3,64]{1,0:T(4,128)}) custom-call(f32[8,64,256]{2,1,0:T(8,128)} %r_in.1, f32[8,64,256]{2,1,0:T(8,128)} %d_in.1, bf16[8,256,256]{2,1,0:T(8,128)(2,1)} %kmat_in.1, bf16[8,256,256]{2,1,0:T(8,128)(2,1)} %dmat_in.1, bf16[8,24,256]{2,1,0:T(8,128)(2,1)} %coupling_in.1, ...), custom_call_target="tpu_custom_call" | custom-call | tf_op jit(solution)/shard_map/pallas_call | solution.py:426
  114.1 1.9 %copy.13 = f32[8,64,256]{2,1,0:T(8,128)} copy(f32[8,64,256]{2,1,0:T(8,128)} %get-tuple-element.6) | data formatting | bytes 1048576
  115.9 1.9 %copy.14 = f32[8,64,256]{2,1,0:T(8,128)} copy(f32[8,64,256]{2,1,0:T(8,128)} %get-tuple-element.7) | data formatting | bytes 1048576
  117.8 1.3 %copy.15 = f32[3,64]{1,0:T(4,128)} copy(f32[3,64]{1,0:T(4,128)} %get-tuple-element.8) | data formatting | bytes 1536

commit v3 on v2

v3 whole, which is shorter than its diff:
```python
import functools

import jax
import jax.numpy as jnp
from jax import lax
from jax.experimental import pallas as pl
from jax.experimental.pallas import tpu as pltpu
from jax.sharding import PartitionSpec as P

ITERS = 3
MESH = pl.DeviceIdType.MESH
F32, BF16 = jnp.float32, jnp.bfloat16
BLK = 256
VMEM_LIMIT = 63 * 1024 * 1024


def nn(a, b):
    return lax.dot_general(a, b, (((1,), (0,)), ((), ())), preferred_element_type=F32)


def nt(a, b):
    return lax.dot_general(a, b, (((1,), (1,)), ((), ())), preferred_element_type=F32)


def pieces(x):
    high = x.astype(BF16)
    return high, (x - high.astype(F32)).astype(BF16)


def iota(shape, dim):
    return lax.broadcasted_iota(jnp.int32, shape, dim)


def kernel(
    n_grp, n_mem,
    r_in, d_in, kmat_in, dmat_in, coupling_in, corner_map, factor,
    r_out, v_out, d_out, rows_ref,
    r_ref, v_ref, d_ref, kmat, dmat, coupling, cst, solved, track, lift, l_ref, xh, xl, oht, mask, a_ref,
    idx, snd, rcv, snd2, rcv2, idx_all, load, nbr, ext, sums, y_new, y_old, ar, energy,
    sem_l, sem_o, sem_i, sem_f, sem_b, sem_n, sem_x, sem_a, sem_e,
):
    subs, q_all, _ = r_in.shape
    corners = coupling_in.shape[1]
    nb = l_ref.shape[0] // BLK
    rows4 = 4 * nb
    n_rows = 3 * rows4
    me, grp = lax.axis_index("mem"), lax.axis_index("grp")
    top = iota((8, 128), 0) < 4
    top2 = iota((8, BLK), 0) < 4
    band = iota((q_all, 128), 1) // 32
    order = [0]
    for near in range(1, n_mem // 2):
        order += [near, n_mem - near]
    order.append(n_mem // 2)
    chunk = min(4, n_mem)
    n_chunks = n_mem // chunk
    even = lax.rem(grp, 2) == 0
    near_step = jnp.where(even, 1, n_grp - 1)
    far_step = jnp.where(even, n_grp - 1, 1)

    def span(u, count):
        return pl.ds(2 * BLK * u, 2 * BLK * count)

    side = lax.rem(grp // 2, 2)
    across = me + 1 - 2 * lax.rem(me, 2)

    def member_at(step):
        return lax.rem(me + step, n_mem)

    def flip(member):
        return member + side * (1 - 2 * lax.rem(member, 2))

    mine = flip(me)

    def same_rows(step):
        other = lax.rem(grp + step, n_grp)
        turn = lax.rem(other // 2, 2) - side
        return {"grp": other, "mem": me + turn * turn * (1 - 2 * lax.rem(me, 2))}

    barrier = pltpu.get_barrier_semaphore()
    for step in range(1, n_mem):
        pl.semaphore_signal(barrier, inc=1, device_id={"mem": member_at(step)}, device_id_type=MESH)
    for step in range(1, n_grp):
        pl.semaphore_signal(barrier, inc=1, device_id=same_rows(step), device_id_type=MESH)

    fetches = [
        pltpu.make_async_copy(src, dst, sem_l.at[number])
        for number, (src, dst) in enumerate(
            [(d_in, v_ref), (kmat_in, kmat), (coupling_in, coupling), (r_in, r_ref), (dmat_in, dmat)]
            + [(factor.at[0, span(u, 1), span(u, 1)], l_ref.at[span(u, 1), span(u, 1)]) for u in range(nb // 2)]
            + [
                (factor.at[0, span(u + 1, nb // 2 - u - 1), span(u, 1)], l_ref.at[span(u + 1, nb // 2 - u - 1), span(u, 1)])
                for u in range(nb // 2 - 1)
            ]
        )
    ]
    for fetch in fetches:
        fetch.start()

    def to_member(src, dst, sem, step):
        return pltpu.make_async_remote_copy(
            src_ref=src, dst_ref=dst, send_sem=sem.at[0, step], recv_sem=sem.at[1, step],
            device_id={"mem": lax.rem(me + step, n_mem)}, device_id_type=MESH,
        )

    def to_group(src, dst, sem, step):
        return pltpu.make_async_remote_copy(
            src_ref=src, dst_ref=dst, send_sem=sem.at[0, step], recv_sem=sem.at[1, step],
            device_id=same_rows(step), device_id_type=MESH,
        )

    def to_neighbour(src, dst, sem, number, step, member):
        return pltpu.make_async_remote_copy(
            src_ref=src, dst_ref=dst, send_sem=sem.at[0, number], recv_sem=sem.at[1, number],
            device_id={"grp": lax.rem(grp + step, n_grp), "mem": member}, device_id_type=MESH,
        )

    def near_load():
        return to_neighbour(load.at[0:rows4], nbr.at[0], sem_n, nb // 2, near_step, me)

    def far_load(u):
        piece = pl.ds(8 * u, 8)
        return to_neighbour(load.at[pl.ds(2 * rows4 + 8 * u, 8)], nbr.at[1, piece], sem_n, u, far_step, across)

    def near_spread():
        return to_neighbour(ext.at[rows4 : 2 * rows4], ext.at[0:rows4], sem_x, nb // 2, near_step, me)

    def far_spread(u):
        return to_neighbour(
            ext.at[pl.ds(rows4 + 8 * u, 8)], ext.at[pl.ds(2 * rows4 + 8 * u, 8)], sem_x, u, far_step, across
        )

    def reduce_start(*rows):
        first = ar.at[0]
        for number, row in enumerate(rows):
            first[pl.ds(me, 1), number : number + 1, :] = row[None]
        for step in reversed(order[1:]):
            to_member(first.at[me], first.at[me], sem_a.at[0], step).start()

    def reduce_middle():
        first, second = ar.at[0], ar.at[1]
        for step in range(1, n_mem):
            to_member(first.at[me], first.at[member_at(n_mem - step)], sem_a.at[0], step).wait()
        second[pl.ds(grp, 1)] = jnp.sum(first[0:n_mem], axis=0)[None]
        for step in range(1, n_grp):
            to_group(second.at[grp], second.at[grp], sem_a.at[1], step).start()

    def reduce_end():
        second = ar.at[1]
        for step in range(1, n_grp):
            to_group(second.at[grp], second.at[lax.rem(grp + n_grp - step, n_grp)], sem_a.at[1], step).wait()
        return jnp.sum(second[0:n_grp], axis=0)

    def energy_start(squares, crosses):
        place = iota((8, 128), 0) == iota((8, 128), 1)
        column = jnp.where(top, jnp.broadcast_to(squares, (8, 128)), jnp.broadcast_to(crosses, (8, 128)))
        energy[pl.ds(grp, 1)] = jnp.sum(jnp.where(place, column, 0.0), axis=0, keepdims=True)[None]
        for step in range(1, n_grp):
            to_group(energy.at[grp], energy.at[grp], sem_e, step).start()

    def energy_end():
        for step in range(1, n_grp):
            to_group(energy.at[grp], energy.at[lax.rem(grp + n_grp - step, n_grp)], sem_e, step).wait()
        row = jnp.sum(energy[...], axis=0)
        place = iota((8, 128), 0) == iota((8, 128), 1)
        column = jnp.sum(jnp.where(place, jnp.broadcast_to(row, (8, 128)), 0.0), axis=1, keepdims=True)
        column = jnp.broadcast_to(column, (8, 128))
        return jnp.where(iota((8, 128), 1) == corners, column, pltpu.roll(column, 4, 0))

    def as_row(*totals):
        spare = 128 - q_all * len(totals)
        fill = [jnp.zeros((spare, BLK), F32)] if spare else []
        wide = jnp.concatenate([*totals, *fill], axis=0)
        first = wide.astype(BF16)
        rest = wide - first.astype(F32)
        second = rest.astype(BF16)
        third = (rest - second.astype(F32)).astype(BF16)
        ones = jnp.ones((8, BLK), BF16)
        out = nt(ones, first) + (nt(ones, second) + nt(ones, third))
        return out[0:1]

    def as_column(row, offset=0):
        diagonal = iota((q_all, 128), 0) + offset == iota((q_all, 128), 1)
        return jnp.sum(jnp.where(diagonal, jnp.broadcast_to(row, (q_all, 128)), 0.0), axis=1, keepdims=True)

    def back_to_row(column):
        diagonal = iota((q_all, 128), 0) == iota((q_all, 128), 1)
        return jnp.sum(jnp.where(diagonal, jnp.broadcast_to(column, (q_all, 128)), 0.0), axis=0, keepdims=True)

    mine4 = iota((8, 128), 1) == 4 * mine + lax.rem(iota((8, 128), 0), 4)

    def as_my_column(row):
        return jnp.sum(jnp.where(mine4, jnp.broadcast_to(row, (8, 128)), 0.0), axis=1, keepdims=True)

    def build_tables():
        cst[...] = jnp.zeros(cst.shape, BF16)
        for s in range(subs):
            cst[s // 4, 32 * (s % 4) : 32 * (s % 4) + corners, :] = coupling[s]
        idx[...] = jnp.full((8, 128), -1, jnp.int32)
        idx[:, 0:corners] = corner_map[...]
        wide = idx[...]
        lane, sub = iota((8, 128), 1) // 32, iota((8, 128), 0)
        tile = jnp.full((8, 128), -1, jnp.int32)
        for s in range(subs):
            turned = pltpu.roll(wide, 32 * (s % 4), 1)[s : s + 1] if s % 4 else wide[s : s + 1]
            tile = jnp.where((lane == s % 4) & (sub // 4 == s // 4), jnp.broadcast_to(turned, (8, 128)), tile)
        idx[...] = tile

    def local_partials():
        halves = []
        for h in range(2):
            stack = []
            for s in range(4 * h, 4 * h + 4):
                out = nn(v_ref[s].astype(BF16), kmat[s])
                solved[s] = out
                stack += pieces(out)
            found = nt(jnp.concatenate(stack, axis=0), cst[h])
            total = jnp.zeros((q_all, 128), F32)
            for s in range(4):
                part = found[2 * s * q_all : (2 * s + 1) * q_all] + found[(2 * s + 1) * q_all : (2 * s + 2) * q_all]
                total = jnp.where(band == s, part, total)
            halves.append(total)
        for v in range(q_all // 8):
            a, b = halves[0][8 * v : 8 * v + 8], halves[1][8 * v : 8 * v + 8]
            snd[2 * v] = jnp.where(top, a, pltpu.roll(b, 4, 0))
            snd[2 * v + 1] = jnp.where(top, pltpu.roll(a, 4, 0), b)

    def send_partials():
        for step in reversed(order[1:]):
            to_member(snd.at[flip(member_at(step))], rcv.at[me], sem_f, step).start()
        rcv[pl.ds(me, 1)] = snd[pl.ds(mine, 1)]

    def block(i, j):
        return l_ref[i * BLK : (i + 1) * BLK, j * BLK : (j + 1) * BLK]

    def triple(left, high, low):
        left_high, left_low = pieces(left)
        return nn(left_high, high) + (nn(left_high, low) + nn(left_low, high))

    half = BLK // 2

    def between(high, low, off, high_after, low_after):
        left = nn(jnp.concatenate([high, low], axis=1), jnp.concatenate([off, off], axis=0))
        left = jnp.concatenate(pieces(left), axis=1)
        after = jnp.concatenate(
            [
                jnp.concatenate([high_after, low_after], axis=1),
                jnp.concatenate([high_after, jnp.zeros_like(low_after)], axis=1),
            ],
            axis=0,
        )
        out = nn(left, after)
        return out[:, :half] + out[:, half:]

    def invert_blocks(first, count):
        row, col = iota((half, half), 0), iota((half, half), 1)
        numbers = range(2 * first, 2 * (first + count))

        def tile(i, j):
            return l_ref[i * half : (i + 1) * half, j * half : (j + 1) * half]

        inverses = []
        for i in numbers:
            tri = tile(i, i).astype(F32)
            diag = jnp.where(row == col, tri, 0.0)
            down = 1.0 / jnp.sum(diag, axis=1, keepdims=True)
            along = 1.0 / jnp.sum(diag, axis=0, keepdims=True)
            below = (row // 2 == col // 2) & (row > col)
            inverses.append(jnp.where(row == col, down, 0.0) - jnp.where(below, tri * down * along, 0.0))
        size = 2
        while size < half:
            below = (row // (2 * size) == col // (2 * size)) & (row // size > col // size)
            split = [pieces(inv) for inv in inverses]
            offs = [jnp.where(below, tile(i, i).astype(F32), 0.0).astype(BF16) for i in numbers]
            inverses = [
                inv - between(*pair, off, *pair) for inv, pair, off in zip(inverses, split, offs)
            ]
            size *= 2
        split = [pieces(inv) for inv in inverses]
        nothing = jnp.zeros((half, half), BF16)
        for number in range(count):
            i = first + number
            before, after = split[2 * number], split[2 * number + 1]
            corner = pieces(-between(*after, tile(2 * i + 1, 2 * i), *before))
            for ref, a, b, c in zip((xh, xl), before, after, corner):
                ref[i // 2, i % 2, :half, :half] = a
                ref[i // 2, i % 2, :half, half:] = nothing
                ref[i // 2, i % 2, half:, :half] = c
                ref[i // 2, i % 2, half:, half:] = b
        for u in range(first // 2, (first + count) // 2):
            off = block(2 * u + 1, 2 * u)
            left = nn(xh[u, 1], off) + nn(xl[u, 1], off)
            xh[u, 2], xl[u, 2] = pieces(-triple(left, xh[u, 0], xl[u, 0]))

    def build_masks():
        for step in range(1, n_mem):
            to_member(idx, idx_all.at[member_at(n_mem - step)], sem_i, step).wait()
        for position, step in enumerate(order):
            tile = idx_all[pl.ds(member_at(n_mem - step), 1)][0]
            for h in range(2):
                line = tile[4 * h : 4 * h + 1]
                at = position * BLK + h * 128
                lo = jnp.broadcast_to(line & (BLK - 1), (BLK, 128))
                oht[:, at : at + 128] = jnp.where(lo == iota((BLK, 128), 0), 1.0, 0.0).astype(BF16)
                below, above = jnp.where(even, 2 * nb, 0), jnp.where(even, 0, 2 * nb)
                hi = line >> 8
                moved = jnp.where(hi < nb, hi + below, jnp.where(hi < 2 * nb, hi, hi - 2 * nb + above))
                hi = jnp.broadcast_to(jnp.where(hi < 0, -1, moved), (n_rows, 128))
                mask[:, at : at + 128] = jnp.where(hi == iota((n_rows, 128), 0) // 4, 1.0, 0.0)

    def gather_chunk(number):
        positions = range(number * chunk, (number + 1) * chunk)
        for position in positions:
            step = order[position]
            if step:
                to_member(snd.at[flip(member_at(step))], rcv.at[member_at(n_mem - step)], sem_f, step).wait()
        for position in positions:
            tile = rcv[pl.ds(member_at(n_mem - order[position]), 1)][0]
            high = tile.astype(BF16).astype(F32)
            for number_of, part in enumerate((high, tile - high)):
                turned = pltpu.roll(part, 4, 0)
                for h in range(2):
                    twice = jnp.where(top, part, turned) if h == 0 else jnp.where(top, turned, part)
                    at = position * BLK + h * 128
                    full = jnp.concatenate([twice] * (n_rows // 8), axis=0) * mask[:, at : at + 128]
                    a_ref[number_of * n_rows : (number_of + 1) * n_rows, at : at + 128] = full.astype(BF16)
        at = slice(number * chunk * BLK, (number + 1) * chunk * BLK)
        total = nt(a_ref[:, at], oht[:, at])
        total = total[:n_rows] + total[n_rows:]
        load[...] = total if number == 0 else load[...] + total

    def twin(x):
        high, low = pieces(x)
        return jnp.where(top2, high.astype(F32), low.astype(F32)).astype(BF16)

    def folded(x):
        return x + pltpu.roll(x, 4, 0)

    def lower():
        acc, taken = [], [None] * nb
        near_load().wait()
        for u in range(nb // 2):
            far_load(u).wait()
            piece = slice(8 * u, 8 * u + 8)
            x = load[rows4 + 8 * u : rows4 + 8 * u + 8] + nbr[0, piece] + nbr[1, piece]
            y = pltpu.roll(x, 4, 0)
            b0, b1 = jnp.where(top2, x, y), jnp.where(top2, y, x)
            if u:
                b0, b1 = b0 - folded(taken[2 * u]), b1 - folded(taken[2 * u + 1])
            p0, p1 = twin(b0), twin(b1)
            y0 = nt(p0, xh[u, 0]) + nt(p0, xl[u, 0])
            y1 = (nt(p0, xh[u, 2]) + nt(p0, xl[u, 2])) + (nt(p1, xh[u, 1]) + nt(p1, xl[u, 1]))
            acc += [folded(y0), folded(y1)]
            p0, p1 = twin(acc[2 * u]), twin(acc[2 * u + 1])
            for t in range(2 * u + 2, nb):
                part = nt(p0, block(t, 2 * u)) + nt(p1, block(t, 2 * u + 1))
                taken[t] = part if taken[t] is None else taken[t] + part
        return acc

    def upper(acc):
        acc = list(acc)
        for u in reversed(range(nb // 2)):
            p0, p1 = twin(acc[2 * u]), twin(acc[2 * u + 1])
            x1 = nn(p1, xh[u, 1]) + nn(p1, xl[u, 1])
            x0 = (nn(p0, xh[u, 0]) + nn(p0, xl[u, 0])) + (nn(p1, xh[u, 2]) + nn(p1, xl[u, 2]))
            x0, x1 = folded(x0), folded(x1)
            ext[rows4 + 8 * u : rows4 + 8 * u + 8] = jnp.where(top2, x0, x1)
            far_spread(u).start()
            p0, p1 = twin(x0), twin(x1)
            for t in range(2 * u):
                acc[t] = acc[t] - folded(nn(p0, block(2 * u, t)) + nn(p1, block(2 * u + 1, t)))
        near_spread().start()

    def pick_rows(role, number):
        rows = slice(role * rows4, (role + 1) * rows4)
        at = slice(number * chunk * BLK, (number + 1) * chunk * BLK)
        high, low = pieces(ext[rows])
        found = nn(jnp.concatenate([high, low], axis=0), oht[:, at])
        found = (found[:rows4] + found[rows4:]) * mask[rows, at]
        total = found[0:8]
        for v in range(1, rows4 // 8):
            total = total + found[8 * v : 8 * v + 8]
        return total

    def pick_early():
        for number in range(n_chunks):
            sums[:, number * chunk * BLK : (number + 1) * chunk * BLK] = pick_rows(1, number)
        near_spread().wait()
        for number in range(n_chunks):
            at = slice(number * chunk * BLK, (number + 1) * chunk * BLK)
            sums[:, at] = sums[:, at] + pick_rows(0, number)

    def pick_chunk(number, extra):
        at = slice(number * chunk * BLK, (number + 1) * chunk * BLK)
        total = sums[:, at] + pick_rows(2, number)
        total = total + pltpu.roll(total, 4, 0)
        steps = []
        padding = top & (iota((8, 128), 1) // 2 == corners // 2)
        for position in range(chunk):
            step = (n_mem - order[number * chunk + position]) % n_mem
            begin = position * BLK
            tile = jnp.where(top, total[:, begin : begin + 128], total[:, begin + 128 : begin + 256])
            tile = jnp.where(padding, extra, tile)
            if step:
                snd2[pl.ds(member_at(step), 1)] = tile[None]
                steps.append(step)
            else:
                rcv2[pl.ds(mine, 1)] = tile[None]
        for step in reversed(steps):
            to_member(snd2.at[member_at(step)], rcv2.at[mine], sem_b, step).start()

    def picked():
        for step in order[1:]:
            to_member(snd2.at[member_at(step)], rcv2.at[flip(member_at(n_mem - step))], sem_b, step).wait()
        halves = ([], [])
        for v in range(q_all // 8):
            a, b = rcv2[2 * v], rcv2[2 * v + 1]
            halves[0].append(jnp.where(top, a, pltpu.roll(b, 4, 0)))
            halves[1].append(jnp.where(top, pltpu.roll(a, 4, 0), b))
        return [jnp.concatenate(half, axis=0) for half in halves]

    def update(halves, alpha, beta):
        total = jnp.zeros((q_all, BLK), F32)
        for h in range(2):
            stack = []
            for s in range(4):
                stack += pieces(jnp.where(band == s, halves[h], 0.0))
            found = nn(jnp.concatenate(stack, axis=0), cst[h])
            for s in range(4):
                lifted = found[2 * s * q_all : (2 * s + 1) * q_all] + found[(2 * s + 1) * q_all : (2 * s + 2) * q_all]
                at = 4 * h + s
                lifted = lifted + beta * lift[at]
                lift[at] = lifted
                image = nn((d_ref[at] + lifted).astype(BF16), kmat[at])
                residual = r_ref[at] - alpha * image
                r_ref[at] = residual
                precond = nn(residual.astype(BF16), dmat[at])
                v_ref[at] = precond
                total = total + residual * precond
        return total

    d_ref[...] = jnp.zeros(d_ref.shape, F32)
    track[...] = jnp.zeros(track.shape, F32)
    lift[...] = jnp.zeros(lift.shape, F32)
    y_old[...] = jnp.zeros(y_old.shape, F32)
    for fetch in fetches[:3]:
        fetch.wait()
    build_tables()
    local_partials()
    for fetch in fetches[3:5]:
        fetch.wait()
    total = jnp.zeros((q_all, BLK), F32)
    for s in range(subs):
        total = total + r_ref[s] * nn(r_ref[s].astype(BF16), dmat[s])
    first_row = as_row(total)
    part = max(2, nb // 2)
    for fetch in fetches[5 : 5 + part // 2]:
        fetch.wait()
    invert_blocks(0, part)
    pl.semaphore_wait(barrier, n_mem + n_grp - 2)
    for step in reversed(order[1:]):
        to_member(idx, idx_all.at[me], sem_i, step).start()
    send_partials()
    idx_all[pl.ds(me, 1)] = idx[...][None]

    def start_sums(norm_row):
        total = jnp.zeros((q_all, BLK), F32)
        mixed = jnp.zeros((q_all, BLK), F32)
        for s in range(subs):
            total = total + v_ref[s] * solved[s]
            mixed = mixed + v_ref[s] * track[s]
        packed = as_row(jnp.zeros((q_all, BLK), F32), total)
        reduce_start(norm_row + packed, as_row(mixed))

    start_sums(first_row)
    for fetch in fetches[5 + part // 2 :]:
        fetch.wait()
    if nb > part:
        invert_blocks(part, nb - part)
    build_masks()

    def iteration(t, before):
        norm_before, curvature_before = before
        for number in range(n_chunks):
            gather_chunk(number)
        for u in range(nb // 2):
            far_load(u).start()
        near_load().start()
        reduce_middle()
        acc = lower()
        squares = jnp.zeros((8, BLK), F32)
        crosses = jnp.zeros((8, BLK), F32)
        for i in range(nb):
            y_new[i] = acc[i]
            squares = squares + acc[i] * acc[i]
            crosses = crosses + acc[i] * y_old[i]
        found = reduce_end()
        energy_start(jnp.sum(squares, axis=1, keepdims=True), jnp.sum(crosses, axis=1, keepdims=True))
        upper(acc)
        pick_early()
        extra = energy_end()
        for u in range(nb // 2):
            far_spread(u).wait()
        for number in reversed(range(n_chunks)):
            pick_chunk(number, extra)
        norm_now = found[0:1]
        beta = jnp.where(t == 0, 0.0, norm_now / norm_before)
        beta_column = as_column(beta)
        my_beta = as_my_column(beta)
        for s in range(subs):
            d_ref[s] = v_ref[s] + beta_column * d_ref[s]
            track[s] = solved[s] + beta_column * track[s]
        for i in range(nb):
            y_old[i] = y_new[i] + my_beta * y_old[i]
        plain = as_column(norm_now, q_all)
        mixed = 2.0 * as_column(found[1:2]) + beta_column * curvature_before
        plain = plain + beta_column * mixed
        norm_column = as_column(norm_now)
        halves = picked()
        curvature = plain + (
            halves[0][:, corners : corners + 1] + 2.0 * beta_column * halves[0][:, corners + 1 : corners + 2]
        )
        alpha = norm_column / curvature
        norm_row = as_row(update(halves, alpha, beta_column))
        rows_ref[pl.ds(t, 1), :] = back_to_row(alpha)

        @pl.when(t < ITERS - 1)
        def _():
            local_partials()
            send_partials()
            start_sums(norm_row)

        @pl.when(t == ITERS - 1)
        def _():
            reduce_start(norm_row)

        return norm_now, curvature

    start = (jnp.ones((1, 128), F32), jnp.zeros((q_all, 1), F32))
    norm_before, _ = lax.fori_loop(0, ITERS, iteration, start)
    leaving = [
        pltpu.make_async_copy(src, dst, sem_o.at[number])
        for number, (src, dst) in enumerate(((r_ref, r_out), (v_ref, v_out), (d_ref, d_out)))
    ]
    for copy in leaving:
        copy.start()
    reduce_middle()
    rows_ref[ITERS : ITERS + 1, :] = reduce_end()[0:1] / norm_before
    for copy in leaving:
        copy.wait()


def finish(r_in, v_in, d_in, rows_in, r_out, d_out, steps_out, r_ref, v_ref, d_ref, rows, sem):
    subs, q_all, _ = r_ref.shape
    copies = [
        pltpu.make_async_copy(src, dst, sem.at[number])
        for number, (src, dst) in enumerate(
            ((v_in, v_ref), (d_in, d_ref), (rows_in, rows), (r_in, r_ref), (r_ref, r_out), (d_ref, d_out))
        )
    ]
    for copy in copies[:4]:
        copy.start()
    for copy in copies[:3]:
        copy.wait()
    diagonal = iota((q_all, 128), 0) == iota((q_all, 128), 1)
    beta = jnp.broadcast_to(rows[ITERS : ITERS + 1, :], (q_all, 128))
    beta = jnp.sum(jnp.where(diagonal, beta, 0.0), axis=1, keepdims=True)
    for s in range(subs):
        d_ref[s] = v_ref[s] + beta * d_ref[s]
    copies[5].start()
    copies[3].wait()
    copies[4].start()
    steps_out[...] = rows[0:ITERS, 0:q_all]
    copies[5].wait()
    copies[4].wait()


def local(n_grp, n_mem, residual, direction, local_inverse, dirichlet, coupling, corner_map, coarse_factor):
    subs, q_all, nr = residual.shape
    order = coarse_factor.shape[1]
    nb = order // BLK
    n_rows = 12 * nb
    most = max(n_mem, n_grp)
    dma = pltpu.SemaphoreType.DMA
    vmem = pl.BlockSpec(memory_space=pltpu.VMEM)
    anywhere = pl.BlockSpec(memory_space=pltpu.HBM)
    field = pltpu.VMEM(residual.shape, F32)
    tiles = pltpu.VMEM((n_mem, 8, 128), F32)
    whole = jax.ShapeDtypeStruct(residual.shape, F32)
    fields = pl.pallas_call(
        functools.partial(kernel, n_grp, n_mem),
        out_shape=(whole, whole, whole, jax.ShapeDtypeStruct((8, 128), F32)),
        in_specs=[anywhere] * 5 + [vmem, anywhere],
        out_specs=(anywhere,) * 3 + (vmem,),
        scratch_shapes=[
            field,
            field,
            field,
            pltpu.VMEM(local_inverse.shape, BF16),
            pltpu.VMEM(dirichlet.shape, BF16),
            pltpu.VMEM(coupling.shape, BF16),
            pltpu.VMEM((2, 128, nr), BF16),
            field,
            field,
            field,
            pltpu.VMEM((order, order), BF16),
            pltpu.VMEM((nb // 2, 3, BLK, BLK), BF16),
            pltpu.VMEM((nb // 2, 3, BLK, BLK), BF16),
            pltpu.VMEM((BLK, n_mem * BLK), BF16),
            pltpu.VMEM((n_rows, n_mem * BLK), F32),
            pltpu.VMEM((2 * n_rows, n_mem * BLK), BF16),
            pltpu.VMEM((8, 128), jnp.int32),
            tiles,
            tiles,
            tiles,
            tiles,
            pltpu.VMEM((n_mem, 8, 128), jnp.int32),
            pltpu.VMEM((n_rows, BLK), F32),
            pltpu.VMEM((2, 4 * nb, BLK), F32),
            pltpu.VMEM((n_rows, BLK), F32),
            pltpu.VMEM((8, n_mem * BLK), F32),
            pltpu.VMEM((nb, 8, BLK), F32),
            pltpu.VMEM((nb, 8, BLK), F32),
            pltpu.VMEM((2, most, 2, 128), F32),
            pltpu.VMEM((n_grp, 1, 128), F32),
            dma((4 + nb,)),
            dma((3,)),
            dma((2, n_mem)),
            dma((2, n_mem)),
            dma((2, n_mem)),
            dma((2, nb // 2 + 1)),
            dma((2, nb // 2 + 1)),
            dma((2, 2, most)),
            dma((2, n_grp)),
        ],
        compiler_params=pltpu.CompilerParams(
            collective_id=0, has_side_effects=True, vmem_limit_bytes=VMEM_LIMIT
        ),
    )(residual, direction, local_inverse, dirichlet, coupling, corner_map, coarse_factor)
    return pl.pallas_call(
        finish,
        out_shape=(whole, whole, jax.ShapeDtypeStruct((ITERS, q_all), F32)),
        in_specs=[anywhere] * 4,
        out_specs=(anywhere, anywhere, vmem),
        scratch_shapes=[field, field, field, pltpu.VMEM((8, 128), F32), dma((6,))],
        compiler_params=pltpu.CompilerParams(vmem_limit_bytes=VMEM_LIMIT),
    )(*fields)


def solution(mesh):
    both = ("grp", "mem")
    return jax.shard_map(
        functools.partial(local, mesh.shape["grp"], mesh.shape["mem"]),
        mesh=mesh,
        in_specs=(P(both), P(both), P(both), P(both), P(both), P(both), P("grp")),
        out_specs=(P(both), P(both), P()),
        check_vma=False,
    )
```

time: 119 us -> 104 us (0.87)
  Pallas kernels: 113 us -> 103 us
  local copies, waits for them, and re-layouts: 4.99 us -> 0 us
    pallas_call x1 -> x2, Pallas kernels: 113 us -> 103 us  [the longest x1 100 us: local(): pl.pallas_call(functools.partial(kernel, n_grp, n_mem), out_shape=(whole,...]
    unnamed x3 -> x0, local copies, waits for them, and re-layouts: 4.99 us -> none
where the time goes in v3:
time: 104 us
  Pallas kernels  103 us (99%)
    pallas_call x1, Pallas kernels, local(): pl.pallas_call(functools.partial(kernel, n_grp, n_mem), out_shape=(whole,...  100 us
    pallas_call x1, Pallas kernels, local(): pl.pallas_call(finish, out_shape=(whole, whole, jax.ShapeDtypeStruct((ITE...  2.93 us

profile of v3, /device:TPU:1, one launch (start us, length us, event | category | flops | bytes accessed | tf_op | source)
XLA Modules:
  0.0 103.7 jit_solution(6854739785319459699)
XLA Ops:
  0.6 100.0 %shard_map.94 = (f32[8,64,256]{2,1,0:T(8,128)}, f32[8,64,256]{2,1,0:T(8,128)}, f32[8,64,256]{2,1,0:T(8,128)}, f32[8,128]{1,0:T(8,128)}) custom-call(f32[8,64,256]{2,1,0:T(8,128)} %r_in.1, f32[8,64,256]{2,1,0:T(8,128)} %d_in.1, bf16[8,256,256]{2,1,0:T(8,128)(2,1)} %kmat_in.1, bf16[8,256,256]{2,1,0:T(8,128)(2,1)} %dmat_in.1, bf16[8,24,256]{2,1,0:T(8,128)(2,1)} %coupling_in.1, ...), custom_call_target="tpu_custom_call" | custom-call | tf_op jit(solution)/shard_map/pallas_call | solution.py:590
  100.7 2.9 %shard_map.95 = (f32[8,64,256]{2,1,0:T(8,128)}, f32[8,64,256]{2,1,0:T(8,128)}, f32[3,64]{1,0:T(4,128)}) custom-call(f32[8,64,256]{2,1,0:T(8,128)} %get-tuple-element.7.r_in, f32[8,64,256]{2,1,0:T(8,128)} %get-tuple-element.8.v_in, f32[8,64,256]{2,1,0:T(8,128)} %get-tuple-element.9.d_in, f32[8,128]{1,0:T(8,128)} %get-tuple-element.10.rows_in), custom_call_target="tpu_custom_call" | custom-call | tf_op jit(solution)/shard_map/pallas_call | solution.py:640

commit v4 on v3

--- a/solution.py
+++ b/solution.py
@@ -11,7 +11,8 @@
 MESH = pl.DeviceIdType.MESH
 F32, BF16 = jnp.float32, jnp.bfloat16
 BLK = 256
-VMEM_LIMIT = 63 * 1024 * 1024
+WIDE = 4
+VMEM_LIMIT = 50 * 1024 * 1024
 
 
 def nn(a, b):
@@ -33,9 +34,9 @@
 
 def kernel(
     n_grp, n_mem,
-    r_in, d_in, kmat_in, dmat_in, coupling_in, corner_map, factor,
+    r_in, d_in, kmat_in, dmat_in, coupling_in, corner_in, factor,
     r_out, v_out, d_out, rows_ref,
-    r_ref, v_ref, d_ref, kmat, dmat, coupling, cst, solved, track, lift, l_ref, xh, xl, oht, mask, a_ref,
+    r_ref, v_ref, d_ref, corner_map, kmat, dmat, coupling, cst, solved, track, lift, l_ref, xh, xl, oht, mask, a_ref,
     idx, snd, rcv, snd2, rcv2, idx_all, load, nbr, ext, sums, y_new, y_old, ar, energy,
     sem_l, sem_o, sem_i, sem_f, sem_b, sem_n, sem_x, sem_a, sem_e,
 ):
@@ -43,6 +44,7 @@
     corners = coupling_in.shape[1]
     nb = l_ref.shape[0] // BLK
     rows4 = 4 * nb
+    wide = min(WIDE, nb)
     n_rows = 3 * rows4
     me, grp = lax.axis_index("mem"), lax.axis_index("grp")
     top = iota((8, 128), 0) < 4
@@ -58,9 +60,6 @@
     near_step = jnp.where(even, 1, n_grp - 1)
     far_step = jnp.where(even, n_grp - 1, 1)
 
-    def span(u, count):
-        return pl.ds(2 * BLK * u, 2 * BLK * count)
-
     side = lax.rem(grp // 2, 2)
     across = me + 1 - 2 * lax.rem(me, 2)
 
@@ -77,16 +76,13 @@
         turn = lax.rem(other // 2, 2) - side
         return {"grp": other, "mem": me + turn * turn * (1 - 2 * lax.rem(me, 2))}
 
-    barrier = pltpu.get_barrier_semaphore()
-    for step in range(1, n_mem):
-        pl.semaphore_signal(barrier, inc=1, device_id={"mem": member_at(step)}, device_id_type=MESH)
-    for step in range(1, n_grp):
-        pl.semaphore_signal(barrier, inc=1, device_id=same_rows(step), device_id_type=MESH)
+    def span(u, count):
+        return pl.ds(2 * BLK * u, 2 * BLK * count)
 
     fetches = [
         pltpu.make_async_copy(src, dst, sem_l.at[number])
         for number, (src, dst) in enumerate(
-            [(d_in, v_ref), (kmat_in, kmat), (coupling_in, coupling), (r_in, r_ref), (dmat_in, dmat)]
+            [(d_in, v_ref), (kmat_in, kmat), (coupling_in, coupling), (corner_in, corner_map), (r_in, r_ref), (dmat_in, dmat)]
             + [(factor.at[0, span(u, 1), span(u, 1)], l_ref.at[span(u, 1), span(u, 1)]) for u in range(nb // 2)]
             + [
                 (factor.at[0, span(u + 1, nb // 2 - u - 1), span(u, 1)], l_ref.at[span(u + 1, nb // 2 - u - 1), span(u, 1)])
@@ -94,8 +90,14 @@
             ]
         )
     ]
-    for fetch in fetches:
+    for fetch in fetches[:4]:
         fetch.start()
+
+    barrier = pltpu.get_barrier_semaphore()
+    for step in range(1, n_mem):
+        pl.semaphore_signal(barrier, inc=1, device_id={"mem": member_at(step)}, device_id_type=MESH)
+    for step in range(1, n_grp):
+        pl.semaphore_signal(barrier, inc=1, device_id=same_rows(step), device_id_type=MESH)
 
     def to_member(src, dst, sem, step):
         return pltpu.make_async_remote_copy(
@@ -130,38 +132,42 @@
             ext.at[pl.ds(rows4 + 8 * u, 8)], ext.at[pl.ds(2 * rows4 + 8 * u, 8)], sem_x, u, far_step, across
         )
 
-    def reduce_start(*rows):
-        first = ar.at[0]
+    def reduce_start(parity, *rows):
+        first = ar.at[parity, 0]
         for number, row in enumerate(rows):
             first[pl.ds(me, 1), number : number + 1, :] = row[None]
         for step in reversed(order[1:]):
-            to_member(first.at[me], first.at[me], sem_a.at[0], step).start()
-
-    def reduce_middle():
-        first, second = ar.at[0], ar.at[1]
+            to_member(first.at[me], first.at[me], sem_a.at[parity, 0], step).start()
+
+    def reduce_middle(parity):
+        first, second = ar.at[parity, 0], ar.at[parity, 1]
         for step in range(1, n_mem):
-            to_member(first.at[me], first.at[member_at(n_mem - step)], sem_a.at[0], step).wait()
+            to_member(first.at[me], first.at[member_at(n_mem - step)], sem_a.at[parity, 0], step).wait()
         second[pl.ds(grp, 1)] = jnp.sum(first[0:n_mem], axis=0)[None]
         for step in range(1, n_grp):
-            to_group(second.at[grp], second.at[grp], sem_a.at[1], step).start()
-
-    def reduce_end():
-        second = ar.at[1]
+            to_group(second.at[grp], second.at[grp], sem_a.at[parity, 1], step).start()
+
+    def reduce_end(parity):
+        second = ar.at[parity, 1]
         for step in range(1, n_grp):
-            to_group(second.at[grp], second.at[lax.rem(grp + n_grp - step, n_grp)], sem_a.at[1], step).wait()
+            source = second.at[lax.rem(grp + n_grp - step, n_grp)]
+            to_group(second.at[grp], source, sem_a.at[parity, 1], step).wait()
         return jnp.sum(second[0:n_grp], axis=0)
 
-    def energy_start(squares, crosses):
+    def energy_start(parity, squares, crosses):
         place = iota((8, 128), 0) == iota((8, 128), 1)
         column = jnp.where(top, jnp.broadcast_to(squares, (8, 128)), jnp.broadcast_to(crosses, (8, 128)))
-        energy[pl.ds(grp, 1)] = jnp.sum(jnp.where(place, column, 0.0), axis=0, keepdims=True)[None]
+        slots = energy.at[parity]
+        slots[pl.ds(grp, 1)] = jnp.sum(jnp.where(place, column, 0.0), axis=0, keepdims=True)[None]
         for step in range(1, n_grp):
-            to_group(energy.at[grp], energy.at[grp], sem_e, step).start()
-
-    def energy_end():
+            to_group(slots.at[grp], slots.at[grp], sem_e.at[parity], step).start()
+
+    def energy_end(parity):
+        slots = energy.at[parity]
         for step in range(1, n_grp):
-            to_group(energy.at[grp], energy.at[lax.rem(grp + n_grp - step, n_grp)], sem_e, step).wait()
-        row = jnp.sum(energy[...], axis=0)
+            source = slots.at[lax.rem(grp + n_grp - step, n_grp)]
+            to_group(slots.at[grp], source, sem_e.at[parity], step).wait()
+        row = jnp.sum(slots[...], axis=0)
         place = iota((8, 128), 0) == iota((8, 128), 1)
         column = jnp.sum(jnp.where(place, jnp.broadcast_to(row, (8, 128)), 0.0), axis=1, keepdims=True)
         column = jnp.broadcast_to(column, (8, 128))
@@ -232,10 +238,6 @@
 
     def block(i, j):
         return l_ref[i * BLK : (i + 1) * BLK, j * BLK : (j + 1) * BLK]
-
-    def triple(left, high, low):
-        left_high, left_low = pieces(left)
-        return nn(left_high, high) + (nn(left_high, low) + nn(left_low, high))
 
     half = BLK // 2
 
@@ -283,14 +285,33 @@
             before, after = split[2 * number], split[2 * number + 1]
             corner = pieces(-between(*after, tile(2 * i + 1, 2 * i), *before))
             for ref, a, b, c in zip((xh, xl), before, after, corner):
-                ref[i // 2, i % 2, :half, :half] = a
-                ref[i // 2, i % 2, :half, half:] = nothing
-                ref[i // 2, i % 2, half:, :half] = c
-                ref[i // 2, i % 2, half:, half:] = b
-        for u in range(first // 2, (first + count) // 2):
-            off = block(2 * u + 1, 2 * u)
-            left = nn(xh[u, 1], off) + nn(xl[u, 1], off)
-            xh[u, 2], xl[u, 2] = pieces(-triple(left, xh[u, 0], xl[u, 0]))
+                ref[i // wide, i % wide, i % wide, :half, :half] = a
+                ref[i // wide, i % wide, i % wide, :half, half:] = nothing
+                ref[i // wide, i % wide, i % wide, half:, :half] = c
+                ref[i // wide, i % wide, i % wide, half:, half:] = b
+
+    def merge_blocks(width):
+        if 2 * width <= wide:
+            for h in range(nb // wide):
+                for low in range(0, wide, 2 * width):
+                    mid, end = low + width, low + 2 * width
+                    inner = {}
+                    for i in range(mid, end):
+                        for j in range(low, mid):
+                            total = None
+                            for k in range(j, mid):
+                                off = block(h * wide + i, h * wide + k)
+                                part = nn(off, xh[h, k, j]) + nn(off, xl[h, k, j])
+                                total = part if total is None else total + part
+                            inner[i, j] = pieces(total)
+                    for i in range(mid, end):
+                        for j in range(low, mid):
+                            total = None
+                            for k in range(mid, i + 1):
+                                high, rest = inner[k, j]
+                                part = nn(xh[h, i, k], high) + (nn(xh[h, i, k], rest) + nn(xl[h, i, k], high))
+                                total = part if total is None else total + part
+                            xh[h, i, j], xl[h, i, j] = pieces(-total)
 
     def build_masks():
         for step in range(1, n_mem):
@@ -336,40 +357,74 @@
     def folded(x):
         return x + pltpu.roll(x, 4, 0)
 
-    def lower():
+    def inverse(i, j):
+        place = (i // wide, i % wide, j % wide)
+        return xh[place], xl[place]
+
+    def both(product, left, i, j):
+        high, low = inverse(i, j)
+        return product(left, high) + product(left, low)
+
+    def lower(wide):
         acc, taken = [], [None] * nb
         near_load().wait()
+        for h in range(nb // wide):
+            base = h * wide
+            right = []
+            for u in range(base // 2, (base + wide) // 2):
+                far_load(u).wait()
+            for u in range(base // 2, (base + wide) // 2):
+                piece = slice(8 * u, 8 * u + 8)
+                x = load[rows4 + 8 * u : rows4 + 8 * u + 8] + nbr[0, piece] + nbr[1, piece]
+                y = pltpu.roll(x, 4, 0)
+                right += [jnp.where(top2, x, y), jnp.where(top2, y, x)]
+            if h:
+                right = [b - folded(taken[base + i]) for i, b in enumerate(right)]
+            right = [twin(b) for b in right]
+            found = []
+            for i in range(wide):
+                total = None
+                for j in range(i + 1):
+                    part = both(nt, right[j], base + i, base + j)
+                    total = part if total is None else total + part
+                found.append(folded(total))
+            acc += found
+            found = [twin(y) for y in found]
+            for t in range(base + wide, nb):
+                for j in range(wide):
+                    part = nt(found[j], block(t, base + j))
+                    taken[t] = part if taken[t] is None else taken[t] + part
+        for i in range(nb):
+            y_new[i] = acc[i]
+
+    def upper(wide):
+        acc = [y_new[i] for i in range(nb)]
+        for h in reversed(range(nb // wide)):
+            base = h * wide
+            right = [twin(acc[base + i]) for i in range(wide)]
+            found = [None] * wide
+            for j in reversed(range(wide)):
+                total = None
+                for i in range(j, wide):
+                    part = both(nn, right[i], base + i, base + j)
+                    total = part if total is None else total + part
+                found[j] = folded(total)
+            for u in range(base // 2, (base + wide) // 2):
+                i = 2 * u - base
+                ext[rows4 + 8 * u : rows4 + 8 * u + 8] = jnp.where(top2, found[i], found[i + 1])
+                far_spread(u).start()
+            found = [twin(x) for x in found]
+            for t in range(base):
+                total = None
+                for j in range(wide):
+                    part = nn(found[j], block(base + j, t))
+                    total = part if total is None else total + part
+                acc[t] = acc[t] - folded(total)
+        near_spread().start()
+
+    def far_wait():
         for u in range(nb // 2):
-            far_load(u).wait()
-            piece = slice(8 * u, 8 * u + 8)
-            x = load[rows4 + 8 * u : rows4 + 8 * u + 8] + nbr[0, piece] + nbr[1, piece]
-            y = pltpu.roll(x, 4, 0)
-            b0, b1 = jnp.where(top2, x, y), jnp.where(top2, y, x)
-            if u:
-                b0, b1 = b0 - folded(taken[2 * u]), b1 - folded(taken[2 * u + 1])
-            p0, p1 = twin(b0), twin(b1)
-            y0 = nt(p0, xh[u, 0]) + nt(p0, xl[u, 0])
-            y1 = (nt(p0, xh[u, 2]) + nt(p0, xl[u, 2])) + (nt(p1, xh[u, 1]) + nt(p1, xl[u, 1]))
-            acc += [folded(y0), folded(y1)]
-            p0, p1 = twin(acc[2 * u]), twin(acc[2 * u + 1])
-            for t in range(2 * u + 2, nb):
-                part = nt(p0, block(t, 2 * u)) + nt(p1, block(t, 2 * u + 1))
-                taken[t] = part if taken[t] is None else taken[t] + part
-        return acc
-
-    def upper(acc):
-        acc = list(acc)
-        for u in reversed(range(nb // 2)):
-            p0, p1 = twin(acc[2 * u]), twin(acc[2 * u + 1])
-            x1 = nn(p1, xh[u, 1]) + nn(p1, xl[u, 1])
-            x0 = (nn(p0, xh[u, 0]) + nn(p0, xl[u, 0])) + (nn(p1, xh[u, 2]) + nn(p1, xl[u, 2]))
-            x0, x1 = folded(x0), folded(x1)
-            ext[rows4 + 8 * u : rows4 + 8 * u + 8] = jnp.where(top2, x0, x1)
-            far_spread(u).start()
-            p0, p1 = twin(x0), twin(x1)
-            for t in range(2 * u):
-                acc[t] = acc[t] - folded(nn(p0, block(2 * u, t)) + nn(p1, block(2 * u + 1, t)))
-        near_spread().start()
+            far_spread(u).wait()
 
     def pick_rows(role, number):
         rows = slice(role * rows4, (role + 1) * rows4)
@@ -419,7 +474,7 @@
             halves[1].append(jnp.where(top, pltpu.roll(a, 4, 0), b))
         return [jnp.concatenate(half, axis=0) for half in halves]
 
-    def update(halves, alpha, beta):
+    def update(halves, alpha, beta, t):
         total = jnp.zeros((q_all, BLK), F32)
         for h in range(2):
             stack = []
@@ -429,7 +484,7 @@
             for s in range(4):
                 lifted = found[2 * s * q_all : (2 * s + 1) * q_all] + found[(2 * s + 1) * q_all : (2 * s + 2) * q_all]
                 at = 4 * h + s
-                lifted = lifted + beta * lift[at]
+                lifted = lifted + jnp.where(t == 0, 0.0, beta * lift[at])
                 lift[at] = lifted
                 image = nn((d_ref[at] + lifted).astype(BF16), kmat[at])
                 residual = r_ref[at] - alpha * image
@@ -439,44 +494,39 @@
                 total = total + residual * precond
         return total
 
-    d_ref[...] = jnp.zeros(d_ref.shape, F32)
-    track[...] = jnp.zeros(track.shape, F32)
-    lift[...] = jnp.zeros(lift.shape, F32)
     y_old[...] = jnp.zeros(y_old.shape, F32)
-    for fetch in fetches[:3]:
+    for fetch in fetches[:4]:
         fetch.wait()
+    for fetch in fetches[4:]:
+        fetch.start()
     build_tables()
     local_partials()
-    for fetch in fetches[3:5]:
-        fetch.wait()
-    total = jnp.zeros((q_all, BLK), F32)
-    for s in range(subs):
-        total = total + r_ref[s] * nn(r_ref[s].astype(BF16), dmat[s])
-    first_row = as_row(total)
     part = max(2, nb // 2)
-    for fetch in fetches[5 : 5 + part // 2]:
-        fetch.wait()
-    invert_blocks(0, part)
     pl.semaphore_wait(barrier, n_mem + n_grp - 2)
     for step in reversed(order[1:]):
         to_member(idx, idx_all.at[me], sem_i, step).start()
     send_partials()
     idx_all[pl.ds(me, 1)] = idx[...][None]
 
-    def start_sums(norm_row):
+    def start_sums(parity, norm, first=False):
         total = jnp.zeros((q_all, BLK), F32)
         mixed = jnp.zeros((q_all, BLK), F32)
         for s in range(subs):
             total = total + v_ref[s] * solved[s]
-            mixed = mixed + v_ref[s] * track[s]
-        packed = as_row(jnp.zeros((q_all, BLK), F32), total)
-        reduce_start(norm_row + packed, as_row(mixed))
-
-    start_sums(first_row)
-    for fetch in fetches[5 + part // 2 :]:
+            if not first:
+                mixed = mixed + v_ref[s] * track[s]
+        reduce_start(parity, as_row(norm, total), as_row(mixed))
+
+    for fetch in fetches[4:6]:
         fetch.wait()
-    if nb > part:
-        invert_blocks(part, nb - part)
+    first_norm = jnp.zeros((q_all, BLK), F32)
+    for s in range(subs):
+        first_norm = first_norm + r_ref[s] * nn(r_ref[s].astype(BF16), dmat[s])
+    start_sums(0, first_norm, True)
+    for fetch in fetches[6:]:
+        fetch.wait()
+    for first in range(0, nb, part):
+        invert_blocks(first, part)
     build_masks()
 
     def iteration(t, before):
@@ -486,30 +536,50 @@
         for u in range(nb // 2):
             far_load(u).start()
         near_load().start()
-        reduce_middle()
-        acc = lower()
+        reduce_middle(lax.rem(t, 2))
+
+        @pl.when(t == 0)
+        def _():
+            merge_blocks(1)
+            lower(2)
+
+        @pl.when(t > 0)
+        def _():
+            lower(wide)
+
         squares = jnp.zeros((8, BLK), F32)
         crosses = jnp.zeros((8, BLK), F32)
         for i in range(nb):
-            y_new[i] = acc[i]
-            squares = squares + acc[i] * acc[i]
-            crosses = crosses + acc[i] * y_old[i]
-        found = reduce_end()
-        energy_start(jnp.sum(squares, axis=1, keepdims=True), jnp.sum(crosses, axis=1, keepdims=True))
-        upper(acc)
+            squares = squares + y_new[i] * y_new[i]
+            crosses = crosses + y_new[i] * y_old[i]
+        energy_start(lax.rem(t, 2), jnp.sum(squares, axis=1, keepdims=True), jnp.sum(crosses, axis=1, keepdims=True))
+
+        @pl.when(t == 0)
+        def _():
+            upper(2)
+
+        @pl.when(t > 0)
+        def _():
+            upper(wide)
+
         pick_early()
-        extra = energy_end()
-        for u in range(nb // 2):
-            far_spread(u).wait()
+        far_wait()
+        extra = energy_end(lax.rem(t, 2))
         for number in reversed(range(n_chunks)):
             pick_chunk(number, extra)
+
+        @pl.when(t == 0)
+        def _():
+            merge_blocks(2)
+
+        found = reduce_end(lax.rem(t, 2))
         norm_now = found[0:1]
         beta = jnp.where(t == 0, 0.0, norm_now / norm_before)
         beta_column = as_column(beta)
         my_beta = as_my_column(beta)
         for s in range(subs):
-            d_ref[s] = v_ref[s] + beta_column * d_ref[s]
-            track[s] = solved[s] + beta_column * track[s]
+            d_ref[s] = v_ref[s] + jnp.where(t == 0, 0.0, beta_column * d_ref[s])
+            track[s] = solved[s] + jnp.where(t == 0, 0.0, beta_column * track[s])
         for i in range(nb):
             y_old[i] = y_new[i] + my_beta * y_old[i]
         plain = as_column(norm_now, q_all)
@@ -521,19 +591,19 @@
             halves[0][:, corners : corners + 1] + 2.0 * beta_column * halves[0][:, corners + 1 : corners + 2]
         )
         alpha = norm_column / curvature
-        norm_row = as_row(update(halves, alpha, beta_column))
-        rows_ref[pl.ds(t, 1), :] = back_to_row(alpha)
+        norm = update(halves, alpha, beta_column, t)
 
         @pl.when(t < ITERS - 1)
         def _():
             local_partials()
             send_partials()
-            start_sums(norm_row)
+            start_sums(lax.rem(t + 1, 2), norm)
 
         @pl.when(t == ITERS - 1)
         def _():
-            reduce_start(norm_row)
-
+            reduce_start(ITERS % 2, as_row(norm))
+
+        rows_ref[pl.ds(t, 1), :] = back_to_row(alpha)
         return norm_now, curvature
 
     start = (jnp.ones((1, 128), F32), jnp.zeros((q_all, 1), F32))
@@ -544,35 +614,26 @@
     ]
     for copy in leaving:
         copy.start()
-    reduce_middle()
-    rows_ref[ITERS : ITERS + 1, :] = reduce_end()[0:1] / norm_before
+    reduce_middle(ITERS % 2)
+    rows_ref[ITERS : ITERS + 1, :] = reduce_end(ITERS % 2)[0:1] / norm_before
     for copy in leaving:
         copy.wait()
 
 
-def finish(r_in, v_in, d_in, rows_in, r_out, d_out, steps_out, r_ref, v_ref, d_ref, rows, sem):
-    subs, q_all, _ = r_ref.shape
-    copies = [
-        pltpu.make_async_copy(src, dst, sem.at[number])
-        for number, (src, dst) in enumerate(
-            ((v_in, v_ref), (d_in, d_ref), (rows_in, rows), (r_in, r_ref), (r_ref, r_out), (d_ref, d_out))
-        )
-    ]
-    for copy in copies[:4]:
-        copy.start()
-    for copy in copies[:3]:
-        copy.wait()
+def finish(r_in, v_in, d_in, rows, r_out, d_out, steps_out, d_ref, sem):
+    subs, q_all, _ = d_ref.shape
+    rest = pltpu.make_async_copy(r_in, r_out, sem.at[0])
+    rest.start()
     diagonal = iota((q_all, 128), 0) == iota((q_all, 128), 1)
     beta = jnp.broadcast_to(rows[ITERS : ITERS + 1, :], (q_all, 128))
     beta = jnp.sum(jnp.where(diagonal, beta, 0.0), axis=1, keepdims=True)
     for s in range(subs):
-        d_ref[s] = v_ref[s] + beta * d_ref[s]
-    copies[5].start()
-    copies[3].wait()
-    copies[4].start()
+        d_ref[s] = v_in[s] + beta * d_in[s]
+    moved = pltpu.make_async_copy(d_ref, d_out, sem.at[1])
+    moved.start()
     steps_out[...] = rows[0:ITERS, 0:q_all]
-    copies[5].wait()
-    copies[4].wait()
+    rest.wait()
+    moved.wait()
 
 
 def local(n_grp, n_mem, residual, direction, local_inverse, dirichlet, coupling, corner_map, coarse_factor):
@@ -585,17 +646,21 @@
     vmem = pl.BlockSpec(memory_space=pltpu.VMEM)
     anywhere = pl.BlockSpec(memory_space=pltpu.HBM)
     field = pltpu.VMEM(residual.shape, F32)
+    wide = min(WIDE, nb)
+    inverse = pltpu.VMEM((nb // wide, wide, wide, BLK, BLK), BF16)
     tiles = pltpu.VMEM((n_mem, 8, 128), F32)
     whole = jax.ShapeDtypeStruct(residual.shape, F32)
+    operands = (residual, direction, local_inverse, dirichlet, coupling, corner_map, coarse_factor)
     fields = pl.pallas_call(
         functools.partial(kernel, n_grp, n_mem),
         out_shape=(whole, whole, whole, jax.ShapeDtypeStruct((8, 128), F32)),
-        in_specs=[anywhere] * 5 + [vmem, anywhere],
+        in_specs=[anywhere] * 7,
         out_specs=(anywhere,) * 3 + (vmem,),
         scratch_shapes=[
             field,
             field,
             field,
+            pltpu.VMEM(corner_map.shape, jnp.int32),
             pltpu.VMEM(local_inverse.shape, BF16),
             pltpu.VMEM(dirichlet.shape, BF16),
             pltpu.VMEM(coupling.shape, BF16),
@@ -604,8 +669,8 @@
             field,
             field,
             pltpu.VMEM((order, order), BF16),
-            pltpu.VMEM((nb // 2, 3, BLK, BLK), BF16),
-            pltpu.VMEM((nb // 2, 3, BLK, BLK), BF16),
+            inverse,
+            inverse,
             pltpu.VMEM((BLK, n_mem * BLK), BF16),
             pltpu.VMEM((n_rows, n_mem * BLK), F32),
             pltpu.VMEM((2 * n_rows, n_mem * BLK), BF16),
@@ -621,28 +686,28 @@
             pltpu.VMEM((8, n_mem * BLK), F32),
             pltpu.VMEM((nb, 8, BLK), F32),
             pltpu.VMEM((nb, 8, BLK), F32),
-            pltpu.VMEM((2, most, 2, 128), F32),
-            pltpu.VMEM((n_grp, 1, 128), F32),
-            dma((4 + nb,)),
+            pltpu.VMEM((2, 2, most, 2, 128), F32),
+            pltpu.VMEM((2, n_grp, 1, 128), F32),
+            dma((5 + nb,)),
             dma((3,)),
             dma((2, n_mem)),
             dma((2, n_mem)),
             dma((2, n_mem)),
             dma((2, nb // 2 + 1)),
             dma((2, nb // 2 + 1)),
-            dma((2, 2, most)),
-            dma((2, n_grp)),
+            dma((2, 2, 2, most)),
+            dma((2, 2, n_grp)),
         ],
         compiler_params=pltpu.CompilerParams(
             collective_id=0, has_side_effects=True, vmem_limit_bytes=VMEM_LIMIT
         ),
-    )(residual, direction, local_inverse, dirichlet, coupling, corner_map, coarse_factor)
+    )(*(pltpu.with_memory_space_constraint(x, pltpu.HBM) for x in operands))
     return pl.pallas_call(
         finish,
         out_shape=(whole, whole, jax.ShapeDtypeStruct((ITERS, q_all), F32)),
-        in_specs=[anywhere] * 4,
+        in_specs=[vmem] * 4,
         out_specs=(anywhere, anywhere, vmem),
-        scratch_shapes=[field, field, field, pltpu.VMEM((8, 128), F32), dma((6,))],
+        scratch_shapes=[field, dma((2,))],
         compiler_params=pltpu.CompilerParams(vmem_limit_bytes=VMEM_LIMIT),
     )(*fields)
 

time: 104 us -> 99.8 us (0.960)
  Pallas kernels: 103 us -> 98.9 us
    pallas_call x1, Pallas kernels: 100 us -> 97.3 us  [local(): pl.pallas_call(functools.partial(kernel, n_grp, n_mem), out_shape=(whole,...]
    pallas_call x1, Pallas kernels: 2.93 us -> 1.57 us  [local(): pl.pallas_call(finish, out_shape=(whole, whole, jax.ShapeDtypeStruct((ITE...]
where the time goes in v4:
time: 99.8 us; the launch traced here: 99.7 us
  Pallas kernels  98.9 us (99%)
    pallas_call x1, Pallas kernels, local(): pl.pallas_call(functools.partial(kernel, n_grp, n_mem), out_shape=(whole,...  97.3 us

profile of v4, /device:TPU:1, one launch (start us, length us, event | category | flops | bytes accessed | tf_op | source)
XLA Modules:
  0.0 99.7 jit_solution(7585410561338764762)
XLA Ops:
  0.6 97.3 %shard_map.94 = (f32[8,64,256]{2,1,0:T(8,128)S(1)}, f32[8,64,256]{2,1,0:T(8,128)S(1)}, f32[8,64,256]{2,1,0:T(8,128)S(1)}, f32[8,128]{1,0:T(8,128)S(1)}) custom-call(f32[8,64,256]{2,1,0:T(8,128)} %r_in.1, f32[8,64,256]{2,1,0:T(8,128)} %d_in.1, bf16[8,256,256]{2,1,0:T(8,128)(2,1)} %kmat_in.1, bf16[8,256,256]{2,1,0:T(8,128)(2,1)} %dmat_in.1, ...), custom_call_target="tpu_custom_call" | custom-call | tf_op jit(solution)/shard_map/pallas_call | solution.py:654
  98.0 1.6 %shard_map.95 = (f32[8,64,256]{2,1,0:T(8,128)}, f32[8,64,256]{2,1,0:T(8,128)}, f32[3,64]{1,0:T(4,128)}) custom-call(f32[8,64,256]{2,1,0:T(8,128)S(1)} %get-tuple-element.7.r_in, f32[8,64,256]{2,1,0:T(8,128)S(1)} %get-tuple-element.8.v_in, f32[8,64,256]{2,1,0:T(8,128)S(1)} %get-tuple-element.9.d_in, f32[8,128]{1,0:T(8,128)S(1)} %get-tuple-element.10.rows), custom_call_target="tpu_custom_call" | custom-call | tf_op jit(solution)/shard_map/pallas_call | solution.py:705
